TPU v7x, 32 devices: a whole 2x2x4 slice. The times are simulated.
32 devices in a mesh: ta: 8 (over z, x), gx: 4 (over y, core).
Axes of the slice: x: 2, y: 2, z: 4, core: 2. Of those that a mesh axis runs over, the one named last changes fastest.
Arguments:
- links: float32 [16, 4, 18, 32, 512], P('ta', None, None, 'gx'), may hold values from -1 to 1, as said below
Outputs:
- spatial_links: float32 [16, 3, 18, 32, 512], P('ta', None, None, 'gx')
- correlator: float32 [16, 3, 32, 512], P('ta', None, 'gx')
Inputs may be any that keep to these rules, and one draw needn't show every extreme that they name: `links`: every link is a special unitary 3 x 3 complex matrix.
All inputs are finite; a program needn't handle non-finite values.
Results may differ from a plain program's by a relative error of at most 0.00023.
Values sent between devices are 32-bit elements; how exact they have to be, the bound alone decides.
No kernel may reach another device: no remote copies, remote signals or barrier semaphores. Data moves between devices by JAX's collectives and lax.ppermute only.
A program may use at most 128 MiB of HBM per device.

v0:
```python
import functools

import jax
import jax.numpy as jnp
from jax import lax
from jax.experimental import pallas as pl
from jax.experimental.pallas import tpu as pltpu
from jax.sharding import PartitionSpec as P

LZ = 32
LANES = 128


def total(terms):
    result = terms[0]
    for term in terms[1:]:
        result = result + term
    return result


def dot(left, right):
    pairs = list(zip(left, right))
    real = total([a[0] * b[0] for a, b in pairs]) - total([a[1] * b[1] for a, b in pairs])
    imag = total([a[0] * b[1] for a, b in pairs] + [a[1] * b[0] for a, b in pairs])
    return real, imag


def dot_conj(left, right):
    pairs = list(zip(left, right))
    real = total([a[0] * b[0] for a, b in pairs] + [a[1] * b[1] for a, b in pairs])
    imag = total([a[1] * b[0] for a, b in pairs]) - total([a[0] * b[1] for a, b in pairs])
    return real, imag


def times(rows, matrix):
    columns = [[matrix[k][j] for k in range(3)] for j in range(3)]
    return [[dot(row, column) for column in columns] for row in rows]


def times_dagger(rows, matrix):
    return [[dot_conj(row, other) for other in matrix] for row in rows]


def complete(rows):
    first, second = rows[0], rows[1]
    third = []
    for j in range(3):
        a, b = (j + 1) % 3, (j + 2) % 3
        ar, ai = first[a]
        br, bi = second[b]
        cr, ci = first[b]
        dr, di = second[a]
        third.append((ar * br - ai * bi - cr * dr + ci * di, cr * di + ci * dr - ar * bi - ai * br))
    return [first, second, third]


def pick(flag, yes, no):
    return [
        [(jnp.where(flag, y[0], n[0]), jnp.where(flag, y[1], n[1])) for y, n in zip(yr, nr)]
        for yr, nr in zip(yes, no)
    ]


def unit_rows(like):
    one, zero = jnp.ones_like(like), jnp.zeros_like(like)
    return [[(one if i == j else zero, zero) for j in range(3)] for i in range(2)]


def trace_real(left, right):
    aa = dot_conj(left[0], right[0])
    bb = dot_conj(left[1], right[1])
    ab = dot_conj(left[0], right[1])
    ba = dot_conj(left[1], right[0])
    third = (aa[0] * bb[0] - aa[1] * bb[1]) - (ab[0] * ba[0] - ab[1] * ba[1])
    return aa[0] + bb[0] + third


def matrix_at(at, rows):
    return [[(at(i * 3 + j), at((rows + i) * 3 + j)) for j in range(3)] for i in range(rows)]


def put(at, matrix):
    rows = len(matrix)
    for i in range(rows):
        for j in range(3):
            at(i * 3 + j, matrix[i][j][0])
            at((rows + i) * 3 + j, matrix[i][j][1])


def state_rows(planes, half):
    return 12 * half * (planes + 1)


def groups(planes, half):
    for block in range(half):
        yield lambda k, block=block: pl.ds((k * half + block) * planes, planes)
    for block in range(half):
        yield lambda k, block=block: pl.ds(12 * half * planes + k * half + block, 1)


def take(ref, rows, base=0):
    return matrix_at(lambda k: ref[pl.ds(rows(k).start + base, rows(k).size), :], 2)


def give(ref, rows, matrix, base=0):
    def at(k, value):
        ref[pl.ds(rows(k).start + base, rows(k).size), :] = value
    put(at, matrix)


def bit_of(step):
    return lax.rem(lax.axis_index("ta") // (1 << step), 2)


def lane_block(c):
    return pl.ds(pl.multiple_of(c * LANES, LANES), LANES)


def block_kernel(half, links_ref, keep_ref, send_ref, rim_ref, across_ref):
    slices, _, planes, cells = links_ref.shape
    blocks = cells // LANES
    own = bit_of(0)
    first = lambda m: [[(v[0][:1], v[1][:1]) for v in row] for row in m]
    for which in range(2):
        for block in range(half):
            c = (own if which == 0 else 1 - own) * half + block
            at = lane_block(c)
            link = lambda t: matrix_at(lambda k: links_ref[t, k, :, at], 3)
            rows = link(0)[:2]
            for t in range(1, slices):
                before = first(link(t - 1)[:2])
                base = 12 * half + 12 * blocks * (t - 1)
                def edge(k, value):
                    rim_ref[pl.ds(base + k * blocks + c, 1), :] = value
                put(edge, before)
                rows = times(rows, link(t))
            main = keep_ref if which == 0 else send_ref
            def tile(k, value):
                main[(k * half + block) * planes:(k * half + block + 1) * planes, :] = value
            put(tile, rows)
            side = rim_ref if which == 0 else across_ref
            def row(k, value):
                side[k * half + block:k * half + block + 1, :] = value
            put(row, first(rows))


def pair_kernel(planes, half, keep_ref, seen_ref, rim_ref, across_ref, block_ref, lower_ref):
    upper = bit_of(0) == 1
    tiles = 12 * half * planes
    for index, rows in enumerate(groups(planes, half)):
        if index < half:
            own, seen = take(keep_ref, rows), take(seen_ref, rows)
        else:
            own, seen = take(rim_ref, rows, -tiles), take(across_ref, rows, -tiles)
        low, high = pick(upper, seen, own), pick(upper, own, seen)
        give(block_ref, rows, times(low, complete(high)))
        give(lower_ref, rows, low)


def combine_kernel(planes, half, step, first, last, *refs):
    refs = list(refs)
    block_ref, seen_ref = refs.pop(0), refs.pop(0)
    prefix_ref = None if first else refs.pop(0)
    lower_ref = refs.pop(0) if last else None
    flag = bit_of(step) == 1
    odd = bit_of(0) == 1
    for rows in groups(planes, half):
        own, seen = take(block_ref, rows), take(seen_ref, rows)
        block = times(pick(flag, seen, own), complete(pick(flag, own, seen)))
        if first:
            prefix = pick(flag, seen, unit_rows(seen[0][0][0]))
        else:
            before = take(prefix_ref, rows)
            prefix = pick(flag, times(seen, complete(before)), before)
        give(refs[0], rows, block)
        if last:
            after = times(prefix, complete(take(lower_ref, rows)))
            give(refs[1], rows, pick(odd, after, prefix))
            give(refs[2], rows, block)
            give(refs[2], rows, pick(odd, prefix, after), state_rows(planes, half))
        else:
            give(refs[1], rows, prefix)


def close(flag, block, prefix, seen):
    poly = times(pick(flag, seen, block), complete(pick(flag, block, seen)))
    return poly, pick(flag, times(seen, complete(prefix)), prefix)


def prepare(planes, half, step, other, links_ref, rim_ref, block, prefix, seen, field_ref, edge_ref):
    slices, cells = links_ref.shape[0], links_ref.shape[-1]
    blocks = cells // LANES
    flag = bit_of(step) == 1
    own = bit_of(0)
    for index, rows in enumerate(groups(planes, half)):
        local = index % half
        c = (1 - own if other else own) * half + local
        poly, gauge = close(flag, block(rows), prefix(rows), seen(rows))
        for t in range(slices + 1):
            if 0 < t < slices:
                if index < half:
                    link = matrix_at(lambda k: links_ref[t - 1, 3, k, :, lane_block(c)], 3)
                else:
                    base = 12 * half + 12 * blocks * (t - 1)
                    link = complete(matrix_at(lambda k: rim_ref[pl.ds(base + k * blocks + c, 1), :], 2))
                gauge = times(gauge, link)
            value = complete(gauge if t < slices else poly)
            def store(k, v):
                if index < half:
                    field_ref[local, 18 * t + k] = v
                else:
                    at = (18 * t + k) * half + local
                    edge_ref[at:at + 1, :] = v
            put(store, value)


def shifted(load, direction, r, edge):
    value = load(r)
    lane = lax.broadcasted_iota(jnp.int32, value.shape, 1)
    if direction == 0:
        row = lax.broadcasted_iota(jnp.int32, value.shape, 0)
        mixed = jnp.where(row == 0, jnp.broadcast_to(edge(r), value.shape), value)
        return pltpu.roll(mixed, value.shape[0] - 1, 0)
    if direction == 1:
        mixed = jnp.where(lane < LZ, load(r + 1), value)
        return pltpu.roll(mixed, LANES - LZ, 1)
    ahead = pltpu.roll(value, LANES - 1, 1)
    around = pltpu.roll(value, LZ - 1, 1)
    return jnp.where(lax.rem(lane, LZ) == LZ - 1, around, ahead)


def outputs(half, jobs, links_ref, fields, edges, spatial_ref, correlator_ref, out_ref, trace_ref, sem):
    slices, cells = links_ref.shape[0], links_ref.shape[-1]
    blocks = cells // LANES
    own = bit_of(0)

    def field(r, k):
        r = r % blocks
        return fields[r // half][r % half, k]

    def edge(r, k):
        at = k * half + r % half
        return edges[r // half][at:at + 1, :]

    started = []
    for job, (r, direction) in enumerate(jobs):
        c = lax.rem(own * half + r, blocks)
        at = lane_block(c)

        def neighbour(base):
            def one(k):
                return shifted(lambda q: field(q, base + k), direction, r, lambda q: edge(q, base + k))
            return matrix_at(one, 3)

        poly = matrix_at(lambda k: field(r, 18 * slices + k), 3)[:2]
        poly_next = neighbour(18 * slices)
        for t in range(slices):
            link = matrix_at(lambda k: links_ref[t, direction, k, :, at], 3)
            gauge = matrix_at(lambda k: field(r, 18 * t + k), 3)[:2]
            moved = complete(times_dagger(times(gauge, link), neighbour(18 * t)))
            def store(k, v):
                out_ref[job, t, k] = v
            put(store, moved)
            trace_ref[job, t] = trace_real(times(poly, moved), times(moved[:2], poly_next))
        for copy in (
            pltpu.make_async_copy(out_ref.at[job], spatial_ref.at[:, direction, :, :, at], sem.at[job, 0]),
            pltpu.make_async_copy(trace_ref.at[job], correlator_ref.at[:, direction, :, at], sem.at[job, 1]),
        ):
            copy.start()
            started.append(copy)
    for copy in started:
        copy.wait()


def jobs_of(half, late):
    early = [(r, d) for r in range(half) for d in (0, 2)] + [(r, 1) for r in range(half - 1)]
    rest = [(half - 1, 1)] + [(r, d) for r in range(half, 2 * half) for d in range(3)]
    return rest if late else early


def early_kernel(planes, half, step, links_ref, block_ref, prefix_ref, seen_ref, rim_ref,
                 spatial_ref, correlator_ref, field_ref, edge_ref, out_ref, trace_ref, sem):
    prepare(planes, half, step, False, links_ref, rim_ref, lambda g: take(block_ref, g),
            lambda g: take(prefix_ref, g), lambda g: take(seen_ref, g), field_ref, edge_ref)
    outputs(half, jobs_of(half, False), links_ref, [field_ref, field_ref], [edge_ref, edge_ref],
            spatial_ref, correlator_ref, out_ref, trace_ref, sem)


def late_kernel(planes, half, step, links_ref, pair_ref, seen_ref, rim_ref, field_ref, edge_ref,
                spatial_in, correlator_in, spatial_ref, correlator_ref,
                field_late, edge_late, out_ref, trace_ref, sem):
    size = state_rows(planes, half)
    prepare(planes, half, step, True, links_ref, rim_ref, lambda g: take(pair_ref, g),
            lambda g: take(pair_ref, g, size), lambda g: take(seen_ref, g), field_late, edge_late)
    outputs(half, jobs_of(half, True), links_ref, [field_ref, field_late], [edge_ref, edge_late],
            spatial_ref, correlator_ref, out_ref, trace_ref, sem)


def in_vmem(count):
    return [pl.BlockSpec(memory_space=pltpu.VMEM)] * count


def anywhere(count):
    return [pl.BlockSpec(memory_space=pl.ANY)] * count


def cost(flops, size):
    return pl.CostEstimate(flops=flops, bytes_accessed=size, transcendentals=0)


def room(mib):
    return pltpu.CompilerParams(vmem_limit_bytes=mib << 20)


def on_device(links):
    slices, _, _, planes, cells = links.shape
    times_ta, parts_gx = lax.axis_size("ta"), lax.axis_size("gx")
    depth = times_ta.bit_length() - 1
    blocks = cells // LANES
    half = blocks // 2
    if times_ta != 1 << depth or depth < 3 or blocks % 2:
        raise ValueError("unsupported sizes")
    f32 = jnp.float32
    shape = lambda *s: jax.ShapeDtypeStruct(s, f32)
    sites = planes * cells
    size = state_rows(planes, half)
    tiles = 12 * half * planes

    def across(x, step):
        return lax.ppermute(x, "ta", [(i, i ^ (1 << step)) for i in range(times_ta)])

    keep, send, rim, side = pl.pallas_call(
        functools.partial(block_kernel, half),
        out_shape=(shape(tiles, LANES), shape(tiles, LANES),
                   shape(12 * half + 12 * blocks * (slices - 1), LANES), shape(12 * half, LANES)),
        in_specs=in_vmem(1),
        out_specs=tuple(in_vmem(4)),
        cost_estimate=cost(200 * sites, 90 * sites),
        compiler_params=room(8),
        name="block_product",
    )(links[:, 3])

    seen = across(send, 0)
    rim = lax.ppermute(rim, "gx", [(i, (i - 1) % parts_gx) for i in range(parts_gx)])
    side = lax.ppermute(
        side, ("ta", "gx"),
        [(i * parts_gx + j, (i ^ 1) * parts_gx + (j - 1) % parts_gx)
         for i in range(times_ta) for j in range(parts_gx)],
    )
    block, lower = pl.pallas_call(
        functools.partial(pair_kernel, planes, half),
        out_shape=(shape(size, LANES), shape(size, LANES)),
        in_specs=in_vmem(4),
        out_specs=tuple(in_vmem(2)),
        cost_estimate=cost(100 * sites, 50 * sites),
        compiler_params=room(8),
        name="pair",
    )(keep, seen, rim, side)

    prefix = None
    for step in range(1, depth - 1):
        first, last = step == 1, step == depth - 2
        seen = across(block, step)
        operands = [block, seen] + ([] if first else [prefix]) + ([lower] if last else [])
        outs = [shape(size, LANES)] * 2 + ([shape(2 * size, LANES)] if last else [])
        block, prefix, *pair = pl.pallas_call(
            functools.partial(combine_kernel, planes, half, step, first, last),
            out_shape=tuple(outs),
            in_specs=in_vmem(len(operands)),
            out_specs=tuple(in_vmem(len(outs))),
            cost_estimate=cost(200 * sites, 100 * sites),
            compiler_params=room(8),
            name="combine",
        )(*operands)

    step = depth - 1
    seen = across(block, step)
    pair = across(pair[0], 0)
    seen_back = across(seen, 0)

    def scratch(count):
        return [pltpu.VMEM((count, slices, 18, planes, LANES), f32),
                pltpu.VMEM((count, slices, planes, LANES), f32),
                pltpu.SemaphoreType.DMA((count, 2))]

    wide = (shape(slices, 3, 18, planes, cells), shape(slices, 3, planes, cells))
    fields = (shape(half, 18 * (slices + 1), planes, LANES), shape(18 * (slices + 1) * half, LANES))
    spatial, correlator, field, edge = pl.pallas_call(
        functools.partial(early_kernel, planes, half, step),
        out_shape=wide + fields,
        in_specs=in_vmem(5),
        out_specs=tuple(anywhere(2) + in_vmem(2)),
        scratch_shapes=scratch(len(jobs_of(half, False))),
        cost_estimate=cost(2000 * sites, 400 * sites),
        compiler_params=room(12),
        name="early",
    )(links, block, prefix, seen, rim)
    return pl.pallas_call(
        functools.partial(late_kernel, planes, half, step),
        out_shape=wide,
        in_specs=in_vmem(6) + anywhere(2),
        out_specs=tuple(anywhere(2)),
        input_output_aliases={6: 0, 7: 1},
        scratch_shapes=[pltpu.VMEM(f.shape, f32) for f in fields] + scratch(len(jobs_of(half, True))),
        cost_estimate=cost(2500 * sites, 600 * sites),
        compiler_params=room(12),
        name="late",
    )(links, pair, seen_back, rim, field, edge, spatial, correlator)


def solution(mesh):
    in_specs = (P("ta", None, None, "gx", None),)
    out_specs = (P("ta", None, None, "gx", None), P("ta", None, "gx", None))
    return jax.shard_map(on_device, mesh=mesh, in_specs=in_specs, out_specs=out_specs, check_vma=False)
```

profile of v0, /device:TPU:0, one launch (start us, length us, event | category | flops | bytes accessed | tf_op | source)
XLA Modules:
  0.0 30.5 jit_solution(3651115776759907880)
XLA Ops:
  0.6 0.0 copy-start
  0.6 1.3 %slice_bitcast_fusion.links_ref = f32[2,18,8,512]{3,2,1,0:T(8,128)S(1)} fusion(f32[2,4,18,8,512]{4,3,2,1,0:T(8,128)} %links_ref.3), kind=kLoop, calls=%fused_computation | loop fusion | bytes 1179648 | tf_op jit(solution)/shard_map/squeeze | solution.py:341
  1.9 0.1 block_product.1
  2.0 3.0 %collective-permute-start = (f32[192,128]{1,0:T(8,128)S(1)}, f32[192,128]{1,0:T(8,128)S(1)}, u32[]{:S(2)}, u32[]{:S(2)}) collective-permute-start(f32[192,128]{1,0:T(8,128)S(1)} %get-tuple-element.16), channel_id=1, source_target_pairs={{0,4},{4,0},{8,12},{12,8},{16,20},{20,16},{24,28},{28,24},{1,5},{5... | collective-permute-start | bytes 294920 | tf_op jit(solution)/shard_map/ppermute | solution.py:330
  5.1 0.7 %collective-permute-start.1 = (f32[72,128]{1,0:T(8,128)S(1)}, f32[72,128]{1,0:T(8,128)S(1)}, u32[]{:S(2)}, u32[]{:S(2)}) collective-permute-start(f32[72,128]{1,0:T(8,128)S(1)} %get-tuple-element.17), channel_id=1, source_target_pairs={{0,3},{1,0},{2,1},{3,2},{4,7},{5,4},{6,5},{7,6},{8,11},{9,8},{10,9... | collective-permute-start | bytes 110600 | tf_op jit(solution)/shard_map/ppermute | solution.py:344
  5.7 0.9 %collective-permute-start.2 = (f32[24,128]{1,0:T(8,128)S(1)}, f32[24,128]{1,0:T(8,128)S(1)}, u32[]{:S(2)}, u32[]{:S(2)}) collective-permute-start(f32[24,128]{1,0:T(8,128)S(1)} %get-tuple-element.18), channel_id=1, source_target_pairs={{0,7},{1,4},{2,5},{3,6},{4,3},{5,0},{6,1},{7,2},{8,15},{9,12},{10,... | collective-permute-start | bytes 36872 | tf_op jit(solution)/shard_map/ppermute | solution.py:345
  6.7 2.2 %collective-permute-done.2.across_ref = f32[24,128]{1,0:T(8,128)S(1)} collective-permute-done((f32[24,128]{1,0:T(8,128)S(1)}, f32[24,128]{1,0:T(8,128)S(1)}, u32[]{:S(2)}, u32[]{:S(2)}) %collective-permute-start.2) | collective-permute-done | bytes 12320 | tf_op jit(solution)/shard_map/ppermute | solution.py:345
  8.9 0.0 collective-permute-done.1.rim_ref
  8.9 0.0 collective-permute-done.seen_ref
  8.9 0.1 pair.1
  9.0 1.6 %collective-permute-start.3 = (f32[216,128]{1,0:T(8,128)S(1)}, f32[216,128]{1,0:T(8,128)S(1)}, u32[]{:S(2)}, u32[]{:S(2)}) collective-permute-start(f32[216,128]{1,0:T(8,128)S(1)} %get-tuple-element.19.refs_0_), channel_id=1, source_target_pairs={{0,8},{4,12},{8,0},{12,4},{16,24},{20,28},{24,16},{28,20},{1,9},{5... | collective-permute-start | bytes 331784 | tf_op jit(solution)/shard_map/ppermute | solution.py:330
  10.6 4.1 %collective-permute-done.3.refs_1_ = f32[216,128]{1,0:T(8,128)S(1)} collective-permute-done((f32[216,128]{1,0:T(8,128)S(1)}, f32[216,128]{1,0:T(8,128)S(1)}, u32[]{:S(2)}, u32[]{:S(2)}) %collective-permute-start.3) | collective-permute-done | bytes 110624 | tf_op jit(solution)/shard_map/ppermute | solution.py:330
  14.8 0.2 combine.1
  15.0 2.7 %collective-permute-start.5 = (f32[216,128]{1,0:T(8,128)S(1)}, f32[216,128]{1,0:T(8,128)S(1)}, u32[]{:S(2)}, u32[]{:S(2)}) collective-permute-start(f32[216,128]{1,0:T(8,128)S(1)} %get-tuple-element.22.block_ref), channel_id=1, source_target_pairs={{0,16},{4,20},{8,24},{12,28},{16,0},{20,4},{24,8},{28,12},{1,17},{... | collective-permute-start | bytes 331784 | tf_op jit(solution)/shard_map/ppermute | solution.py:330
  17.7 1.1 %collective-permute-start.4 = (f32[432,128]{1,0:T(8,128)S(1)}, f32[432,128]{1,0:T(8,128)S(1)}, u32[]{:S(2)}, u32[]{:S(2)}) collective-permute-start(f32[432,128]{1,0:T(8,128)S(1)} %get-tuple-element.21), channel_id=1, source_target_pairs={{0,4},{4,0},{8,12},{12,8},{16,20},{20,16},{24,28},{28,24},{1,5},{5... | collective-permute-start | bytes 663560 | tf_op jit(solution)/shard_map/ppermute | solution.py:330
  18.7 4.4 %collective-permute-done.5.seen_ref = f32[216,128]{1,0:T(8,128)S(1)} collective-permute-done((f32[216,128]{1,0:T(8,128)S(1)}, f32[216,128]{1,0:T(8,128)S(1)}, u32[]{:S(2)}, u32[]{:S(2)}) %collective-permute-start.5) | collective-permute-done | bytes 110624 | tf_op jit(solution)/shard_map/ppermute | solution.py:330
  23.2 1.2 %collective-permute-start.6 = (f32[216,128]{1,0:T(8,128)S(1)}, f32[216,128]{1,0:T(8,128)S(1)}, u32[]{:S(2)}, u32[]{:S(2)}) collective-permute-start(f32[216,128]{1,0:T(8,128)S(1)} %collective-permute-done.5.seen_ref), channel_id=1, source_target_pairs={{0,4},{4,0},{8,12},{12,8},{16,20},{20,16},{24,28},{28,24},{1,5},{5... | collective-permute-start | bytes 331784 | tf_op jit(solution)/shard_map/ppermute | solution.py:330
  24.4 0.0 copy-done
  24.4 2.3 %early.1 = (f32[2,3,18,8,512]{4,3,2,1,0:T(8,128)}, f32[2,3,8,512]{3,2,1,0:T(8,128)}, f32[2,54,8,128]{3,2,1,0:T(8,128)S(1)}, f32[108,128]{1,0:T(8,128)S(1)}) custom-call(f32[2,4,18,8,512]{4,3,2,1,0:T(8,128)S(1)} %copy-done, f32[216,128]{1,0:T(8,128)S(1)} %get-tuple-element.22.block_ref, f32[216,128]{1,0:T(8,128)S(1)} %get-tuple-element.23.prefix_ref, ...), custom_call_target="tpu_custom_call" | custom-call | flops 8192000 | bytes 1638400 | tf_op jit(solution)/shard_map/early/pallas_call | solution.py:388
  26.8 1.2 %collective-permute-done.6.seen_ref = f32[216,128]{1,0:T(8,128)S(1)} collective-permute-done((f32[216,128]{1,0:T(8,128)S(1)}, f32[216,128]{1,0:T(8,128)S(1)}, u32[]{:S(2)}, u32[]{:S(2)}) %collective-permute-start.6) | collective-permute-done | bytes 110624 | tf_op jit(solution)/shard_map/ppermute | solution.py:330
  27.9 0.0 collective-permute-done.4.pair_ref
  27.9 2.6 %late.1 = (f32[2,3,18,8,512]{4,3,2,1,0:T(8,128)}, f32[2,3,8,512]{3,2,1,0:T(8,128)}) custom-call(f32[2,4,18,8,512]{4,3,2,1,0:T(8,128)S(1)} %copy-done, f32[432,128]{1,0:T(8,128)S(1)} %collective-permute-done.4.pair_ref, f32[216,128]{1,0:T(8,128)S(1)} %collective-permute-done.6.seen_ref, ...), custom_call_target="tpu_custom_call", output_to_operand_aliasing={{0}: (6, {}), {1}: (7, {})} | custom-call | flops 10240000 | bytes 2457600 | tf_op jit(solution)/shard_map/late/pallas_call | solution.py:398
Async XLA Ops:
  0.6 23.8 %copy-start = (f32[2,4,18,8,512]{4,3,2,1,0:T(8,128)S(1)}, f32[2,4,18,8,512]{4,3,2,1,0:T(8,128)}, u32[]{:S(2)}) copy-start(f32[2,4,18,8,512]{4,3,2,1,0:T(8,128)} %links_ref.3) | copy-start | bytes 7077892
  2.0 6.8 %collective-permute-start = (f32[192,128]{1,0:T(8,128)S(1)}, f32[192,128]{1,0:T(8,128)S(1)}, u32[]{:S(2)}, u32[]{:S(2)}) collective-permute-start(f32[192,128]{1,0:T(8,128)S(1)} %get-tuple-element.16), channel_id=1, source_target_pairs={{0,4},{4,0},{8,12},{12,8},{16,20},{20,16},{24,28},{28,24},{1,5},{5... | collective-permute-start | bytes 294920 | tf_op jit(solution)/shard_map/ppermute | solution.py:330
  5.1 3.8 %collective-permute-start.1 = (f32[72,128]{1,0:T(8,128)S(1)}, f32[72,128]{1,0:T(8,128)S(1)}, u32[]{:S(2)}, u32[]{:S(2)}) collective-permute-start(f32[72,128]{1,0:T(8,128)S(1)} %get-tuple-element.17), channel_id=1, source_target_pairs={{0,3},{1,0},{2,1},{3,2},{4,7},{5,4},{6,5},{7,6},{8,11},{9,8},{10,9... | collective-permute-start | bytes 110600 | tf_op jit(solution)/shard_map/ppermute | solution.py:344
  5.7 3.1 %collective-permute-start.2 = (f32[24,128]{1,0:T(8,128)S(1)}, f32[24,128]{1,0:T(8,128)S(1)}, u32[]{:S(2)}, u32[]{:S(2)}) collective-permute-start(f32[24,128]{1,0:T(8,128)S(1)} %get-tuple-element.18), channel_id=1, source_target_pairs={{0,7},{1,4},{2,5},{3,6},{4,3},{5,0},{6,1},{7,2},{8,15},{9,12},{10,... | collective-permute-start | bytes 36872 | tf_op jit(solution)/shard_map/ppermute | solution.py:345
  9.0 5.8 %collective-permute-start.3 = (f32[216,128]{1,0:T(8,128)S(1)}, f32[216,128]{1,0:T(8,128)S(1)}, u32[]{:S(2)}, u32[]{:S(2)}) collective-permute-start(f32[216,128]{1,0:T(8,128)S(1)} %get-tuple-element.19.refs_0_), channel_id=1, source_target_pairs={{0,8},{4,12},{8,0},{12,4},{16,24},{20,28},{24,16},{28,20},{1,9},{5... | collective-permute-start | bytes 331784 | tf_op jit(solution)/shard_map/ppermute | solution.py:330
  15.0 8.2 %collective-permute-start.5 = (f32[216,128]{1,0:T(8,128)S(1)}, f32[216,128]{1,0:T(8,128)S(1)}, u32[]{:S(2)}, u32[]{:S(2)}) collective-permute-start(f32[216,128]{1,0:T(8,128)S(1)} %get-tuple-element.22.block_ref), channel_id=1, source_target_pairs={{0,16},{4,20},{8,24},{12,28},{16,0},{20,4},{24,8},{28,12},{1,17},{... | collective-permute-start | bytes 331784 | tf_op jit(solution)/shard_map/ppermute | solution.py:330
  17.7 10.3 %collective-permute-start.4 = (f32[432,128]{1,0:T(8,128)S(1)}, f32[432,128]{1,0:T(8,128)S(1)}, u32[]{:S(2)}, u32[]{:S(2)}) collective-permute-start(f32[432,128]{1,0:T(8,128)S(1)} %get-tuple-element.21), channel_id=1, source_target_pairs={{0,4},{4,0},{8,12},{12,8},{16,20},{20,16},{24,28},{28,24},{1,5},{5... | collective-permute-start | bytes 663560 | tf_op jit(solution)/shard_map/ppermute | solution.py:330
  23.2 4.7 %collective-permute-start.6 = (f32[216,128]{1,0:T(8,128)S(1)}, f32[216,128]{1,0:T(8,128)S(1)}, u32[]{:S(2)}, u32[]{:S(2)}) collective-permute-start(f32[216,128]{1,0:T(8,128)S(1)} %collective-permute-done.5.seen_ref), channel_id=1, source_target_pairs={{0,4},{4,0},{8,12},{12,8},{16,20},{20,16},{24,28},{28,24},{1,5},{5... | collective-permute-start | bytes 331784 | tf_op jit(solution)/shard_map/ppermute | solution.py:330
where the time goes:
time: 30.7 us; the launch traced here: 30.5 us
  waiting for transfers between devices  11.9 us (39%)
  starting transfers between devices  11.3 us (37%)
  Pallas kernels  5.44 us (18%)
  local copies, waits for them, and re-layouts  1.26 us (4%)
  between operations  0.67 us (2%)
    ppermute x5, waiting for transfers between devices, across(): return lax.ppermute(x, 'ta', [(i, i ^ 1 << step) for i in range(times_ta)])  9.71 us
    ppermute x5, starting transfers between devices, across(): return lax.ppermute(x, 'ta', [(i, i ^ 1 << step) for i in range(times_ta)])  9.66 us
    pallas_call x1, Pallas kernels, on_device(): pl.pallas_call(functools.partial(late_kernel, planes, half, step), out_sh...  2.62 us
    pallas_call x1, Pallas kernels, on_device(): pl.pallas_call(functools.partial(early_kernel, planes, half, step), out_s...  2.33 us
    ppermute x1, waiting for transfers between devices, on_device(): lax.ppermute(side, ('ta', 'gx'), [(i * parts_gx + j, (i ^ 1) * parts_gx +...  2.19 us
    squeeze x1, local copies, waits for them, and re-layouts, on_device(): links[:, 3]  1.26 us
    ppermute x1, starting transfers between devices, on_device(): lax.ppermute(side, ('ta', 'gx'), [(i * parts_gx + j, (i ^ 1) * parts_gx +...  0.93 us
    ppermute x1, starting transfers between devices, on_device(): lax.ppermute(rim, 'gx', [(i, (i - 1) % parts_gx) for i in range(parts_gx)])  0.68 us
  transfers between devices with their start and end apart: 7, of which 4 were waited for; matrix products, arithmetic and copies ran while one was open for 0% of the time, Pallas kernels for 8%

commit v1 on v0

v1 whole, which is shorter than its diff:
```python
import functools

import jax
import jax.numpy as jnp
from jax import lax
from jax.experimental import pallas as pl
from jax.experimental.pallas import tpu as pltpu
from jax.sharding import PartitionSpec as P

LZ = 32
LANES = 128


def total(terms):
    result = terms[0]
    for term in terms[1:]:
        result = result + term
    return result


def dot(left, right):
    pairs = list(zip(left, right))
    real = total([a[0] * b[0] for a, b in pairs]) - total([a[1] * b[1] for a, b in pairs])
    imag = total([a[0] * b[1] for a, b in pairs] + [a[1] * b[0] for a, b in pairs])
    return real, imag


def dot_conj(left, right):
    pairs = list(zip(left, right))
    real = total([a[0] * b[0] for a, b in pairs] + [a[1] * b[1] for a, b in pairs])
    imag = total([a[1] * b[0] for a, b in pairs]) - total([a[0] * b[1] for a, b in pairs])
    return real, imag


def times(rows, matrix):
    columns = [[matrix[k][j] for k in range(3)] for j in range(3)]
    return [[dot(row, column) for column in columns] for row in rows]


def times_dagger(rows, matrix):
    return [[dot_conj(row, other) for other in matrix] for row in rows]


def complete(rows):
    first, second = rows[0], rows[1]
    third = []
    for j in range(3):
        a, b = (j + 1) % 3, (j + 2) % 3
        ar, ai = first[a]
        br, bi = second[b]
        cr, ci = first[b]
        dr, di = second[a]
        third.append((ar * br - ai * bi - cr * dr + ci * di, cr * di + ci * dr - ar * bi - ai * br))
    return [first, second, third]


def pick(flag, yes, no):
    return [
        [(jnp.where(flag, y[0], n[0]), jnp.where(flag, y[1], n[1])) for y, n in zip(yr, nr)]
        for yr, nr in zip(yes, no)
    ]


def unit_rows(like):
    one, zero = jnp.ones_like(like), jnp.zeros_like(like)
    return [[(one if i == j else zero, zero) for j in range(3)] for i in range(2)]


def trace_of_product(left, right):
    reals = total([left[i][j][0] * right[j][i][0] for i in range(3) for j in range(3)])
    return reals - total([left[i][j][1] * right[j][i][1] for i in range(3) for j in range(3)])


def matrix_at(at, rows):
    return [[(at(i * 3 + j), at((rows + i) * 3 + j)) for j in range(3)] for i in range(rows)]


def put(at, matrix):
    rows = len(matrix)
    for i in range(rows):
        for j in range(3):
            at(i * 3 + j, matrix[i][j][0])
            at((rows + i) * 3 + j, matrix[i][j][1])


def groups(planes, half):
    return [lambda k, block=block: pl.ds((k * half + block) * planes, planes) for block in range(half)]


def edge_groups(planes, half):
    return [lambda k, block=block: pl.ds((k * half + block) * planes, 1) for block in range(half)]


def take(ref, rows, base=0):
    return matrix_at(lambda k: ref[pl.ds(rows(k).start + base, rows(k).size), :], 2)


def give(ref, rows, matrix, base=0):
    def at(k, value):
        ref[pl.ds(rows(k).start + base, rows(k).size), :] = value
    put(at, matrix)


def bit_of(step):
    return lax.rem(lax.axis_index("ta") // (1 << step), 2)


def lane_block(c):
    return pl.ds(pl.multiple_of(c * LANES, LANES), LANES)


def block_kernel(half, links_ref, keep_ref, send_ref, raw_ref):
    slices, _, planes, cells = links_ref.shape
    blocks = cells // LANES
    own = bit_of(0)
    for which in range(2):
        for block in range(half):
            c = (own if which == 0 else 1 - own) * half + block
            at = lane_block(c)
            link = lambda t: matrix_at(lambda k: links_ref[t, k, :, at], 3)
            rows = link(0)[:2]
            for t in range(1, slices):
                def edge(k, value):
                    raw_ref[pl.ds((12 * (t - 1) + k) * blocks + c, 1), :] = value
                put(edge, [[(v[0][:1], v[1][:1]) for v in row] for row in link(t - 1)[:2]])
                rows = times(rows, link(t))
            give(keep_ref if which == 0 else send_ref, groups(planes, half)[block], rows)


def pair_kernel(planes, half, keep_ref, seen_ref, block_ref, lower_ref):
    upper = bit_of(0) == 1
    for rows in groups(planes, half):
        own, seen = take(keep_ref, rows), take(seen_ref, rows)
        low, high = pick(upper, seen, own), pick(upper, own, seen)
        give(block_ref, rows, times(low, complete(high)))
        give(lower_ref, rows, low)


def combine_kernel(planes, half, step, first, last, *refs):
    refs = list(refs)
    block_ref, seen_ref = refs.pop(0), refs.pop(0)
    prefix_ref = None if first else refs.pop(0)
    lower_ref = refs.pop(0) if last else None
    flag = bit_of(step) == 1
    odd = bit_of(0) == 1
    for rows in groups(planes, half):
        own, seen = take(block_ref, rows), take(seen_ref, rows)
        block = times(pick(flag, seen, own), complete(pick(flag, own, seen)))
        if first:
            prefix = pick(flag, seen, unit_rows(seen[0][0][0]))
        else:
            before = take(prefix_ref, rows)
            prefix = pick(flag, times(seen, complete(before)), before)
        give(refs[0], rows, block)
        if last:
            after = times(prefix, complete(take(lower_ref, rows)))
            give(refs[1], rows, pick(odd, after, prefix))
            give(refs[2], rows, block)
            give(refs[2], rows, pick(odd, prefix, after), 12 * half * planes)
        else:
            give(refs[1], rows, prefix)


def close(flag, block, prefix, seen):
    poly = times(pick(flag, seen, block), complete(pick(flag, block, seen)))
    return poly, pick(flag, times(seen, complete(prefix)), prefix)


def edge_kernel(planes, half, step, block_ref, prefix_ref, pair_ref, seen_ref, raw_ref, here_ref, side_ref):
    flag = bit_of(step) == 1
    rows_of = 12 * half
    for index, rows in enumerate(edge_groups(planes, half)):
        poly, prefix = close(flag, take(block_ref, rows), take(prefix_ref, rows), take(seen_ref, rows))
        partner = take(pair_ref, rows, rows_of * planes)
        partner = pick(flag, times(take(seen_ref, rows), complete(partner)), partner)
        row = lambda k: pl.ds(k * half + index, 1)
        for ref, gauge in ((here_ref, prefix), (side_ref, partner)):
            give(ref, row, poly)
            give(ref, row, gauge, rows_of)
    here_ref[2 * rows_of:, :] = raw_ref[...]


def prepare(planes, half, step, other, links_ref, block, prefix, seen, field_ref):
    slices = links_ref.shape[0]
    flag = bit_of(step) == 1
    own = bit_of(0)
    for local, rows in enumerate(groups(planes, half)):
        at = lane_block((1 - own if other else own) * half + local)
        poly, gauge = close(flag, block(rows), prefix(rows), seen(rows))
        for t in range(slices + 1):
            if 0 < t < slices:
                gauge = times(gauge, matrix_at(lambda k: links_ref[t - 1, 3, k, :, at], 3))
            def store(k, v):
                field_ref[local, 18 * t + k] = v
            put(store, complete(gauge if t < slices else poly))


def prepare_edge(half, slices, blocks, other, edge_ref, raw_ref, out_ref):
    rows_of = 12 * half
    own = bit_of(0)
    start = (1 - own if other else own) * half
    rows = lambda k: pl.ds(k * half, half)
    poly, gauge = take(edge_ref, rows), take(edge_ref, rows, rows_of)
    for t in range(slices + 1):
        if 0 < t < slices:
            base = 2 * rows_of + 12 * blocks * (t - 1)
            link = matrix_at(lambda k: raw_ref[pl.ds(base + k * blocks + start, half), :], 2)
            gauge = times(gauge, complete(link))
        def store(k, v):
            out_ref[pl.ds((18 * t + k) * half, half), :] = v
        put(store, complete(gauge if t < slices else poly))


def shifted(load, direction, r, edge):
    value = load(r)
    lane = lax.broadcasted_iota(jnp.int32, value.shape, 1)
    if direction == 0:
        row = lax.broadcasted_iota(jnp.int32, value.shape, 0)
        mixed = jnp.where(row == 0, jnp.broadcast_to(edge(r), value.shape), value)
        return pltpu.roll(mixed, value.shape[0] - 1, 0)
    if direction == 1:
        mixed = jnp.where(lane < LZ, load(r + 1), value)
        return pltpu.roll(mixed, LANES - LZ, 1)
    ahead = pltpu.roll(value, LANES - 1, 1)
    around = pltpu.roll(value, LZ - 1, 1)
    return jnp.where(lax.rem(lane, LZ) == LZ - 1, around, ahead)


def outputs(half, jobs, links_ref, fields, edges, out_ref, trace_ref, done):
    slices, cells = links_ref.shape[0], links_ref.shape[-1]
    blocks = cells // LANES
    own = bit_of(0)

    def field(r, k):
        r = r % blocks
        return fields[r // half][r % half, k]

    def edge(r, k):
        at = k * half + r % half
        return edges[r // half][at:at + 1, :]

    for job, (r, direction) in enumerate(jobs):
        at = lane_block(lax.rem(own * half + r, blocks))

        def neighbour(base):
            def one(k):
                return shifted(lambda q: field(q, base + k), direction, r, lambda q: edge(q, base + k))
            return matrix_at(one, 3)

        poly = matrix_at(lambda k: field(r, 18 * slices + k), 3)
        poly_next = neighbour(18 * slices)
        for t in range(slices):
            link = matrix_at(lambda k: links_ref[t, direction, k, :, at], 3)
            gauge = matrix_at(lambda k: field(r, 18 * t + k), 3)[:2]
            moved = complete(times_dagger(times(gauge, link), neighbour(18 * t)))
            def store(k, v):
                out_ref[job, t, k] = v
            put(store, moved)
            around = complete(times_dagger(times_dagger(moved[:2], poly_next), moved))
            trace_ref[job, t] = trace_of_product(poly, around)
        done(job)


def copies(half, jobs, out_ref, trace_ref, spatial_ref, correlator_ref, sem, job):
    r, direction = jobs[job]
    at = lane_block(lax.rem(bit_of(0) * half + r, 2 * half))
    return (
        pltpu.make_async_copy(out_ref.at[job], spatial_ref.at[:, direction, :, :, at], sem.at[job, 0]),
        pltpu.make_async_copy(trace_ref.at[job], correlator_ref.at[:, direction, :, at], sem.at[job, 1]),
    )


def jobs_of(half, late):
    early = [(r, 2) for r in range(half)] + [(r, 1) for r in range(half - 1)]
    rest = [(r, d) for r in range(2 * half) for d in range(3) if (r, d) not in early]
    return rest if late else early


def early_kernel(planes, half, step, links_ref, block_ref, prefix_ref, seen_ref, field_ref, out_ref, trace_ref):
    prepare(planes, half, step, False, links_ref, lambda g: take(block_ref, g),
            lambda g: take(prefix_ref, g), lambda g: take(seen_ref, g), field_ref)
    outputs(half, jobs_of(half, False), links_ref, [field_ref, field_ref], None, out_ref, trace_ref, lambda job: None)


def late_kernel(planes, half, step, links_ref, pair_ref, seen_ref, here_ref, side_ref, field_ref, out_early,
                trace_early, spatial_ref, correlator_ref, field_late, edge_own, edge_late, out_ref, trace_ref,
                sem_early, sem):
    slices, blocks = links_ref.shape[0], links_ref.shape[-1] // LANES
    first = functools.partial(copies, half, jobs_of(half, False), out_early, trace_early,
                              spatial_ref, correlator_ref, sem_early)
    second = functools.partial(copies, half, jobs_of(half, True), out_ref, trace_ref,
                               spatial_ref, correlator_ref, sem)
    for job in range(len(jobs_of(half, False))):
        for copy in first(job):
            copy.start()
    size = 12 * half * planes
    prepare(planes, half, step, True, links_ref, lambda g: take(pair_ref, g),
            lambda g: take(pair_ref, g, size), lambda g: take(seen_ref, g), field_late)
    prepare_edge(half, slices, blocks, False, here_ref, here_ref, edge_own)
    prepare_edge(half, slices, blocks, True, side_ref, here_ref, edge_late)

    def done(job):
        for copy in second(job):
            copy.start()

    outputs(half, jobs_of(half, True), links_ref, [field_ref, field_late], [edge_own, edge_late],
            out_ref, trace_ref, done)
    for count, make in ((len(jobs_of(half, False)), first), (len(jobs_of(half, True)), second)):
        for job in range(count):
            for copy in make(job):
                copy.wait()


def in_vmem(count):
    return [pl.BlockSpec(memory_space=pltpu.VMEM)] * count


def anywhere(count):
    return [pl.BlockSpec(memory_space=pl.ANY)] * count


def cost(flops, size):
    return pl.CostEstimate(flops=flops, bytes_accessed=size, transcendentals=0)


def room(mib):
    return pltpu.CompilerParams(vmem_limit_bytes=mib << 20)


def on_device(links):
    slices, _, _, planes, cells = links.shape
    times_ta, parts_gx = lax.axis_size("ta"), lax.axis_size("gx")
    depth = times_ta.bit_length() - 1
    blocks = cells // LANES
    half = blocks // 2
    if times_ta != 1 << depth or depth < 3 or blocks % 2:
        raise ValueError("unsupported sizes")
    f32 = jnp.float32
    shape = lambda *s: jax.ShapeDtypeStruct(s, f32)
    sites = planes * cells
    size = 12 * half * planes
    raw_rows = 12 * blocks * (slices - 1)

    def across(x, step):
        return lax.ppermute(x, "ta", [(i, i ^ (1 << step)) for i in range(times_ta)])

    keep, send, raw = pl.pallas_call(
        functools.partial(block_kernel, half),
        out_shape=(shape(size, LANES), shape(size, LANES), shape(max(raw_rows, 8), LANES)),
        in_specs=in_vmem(1),
        out_specs=tuple(in_vmem(3)),
        cost_estimate=cost(200 * sites, 90 * sites),
        compiler_params=room(8),
        name="block_product",
    )(links[:, 3])

    seen = across(send, 0)
    block, lower = pl.pallas_call(
        functools.partial(pair_kernel, planes, half),
        out_shape=(shape(size, LANES), shape(size, LANES)),
        in_specs=in_vmem(2),
        out_specs=tuple(in_vmem(2)),
        cost_estimate=cost(100 * sites, 50 * sites),
        compiler_params=room(8),
        name="pair",
    )(keep, seen)

    prefix = None
    for step in range(1, depth - 1):
        first, last = step == 1, step == depth - 2
        seen = across(block, step)
        operands = [block, seen] + ([] if first else [prefix]) + ([lower] if last else [])
        outs = [shape(size, LANES)] * 2 + ([shape(2 * size, LANES)] if last else [])
        block, prefix, *pair = pl.pallas_call(
            functools.partial(combine_kernel, planes, half, step, first, last),
            out_shape=tuple(outs),
            in_specs=in_vmem(len(operands)),
            out_specs=tuple(in_vmem(len(outs))),
            cost_estimate=cost(200 * sites, 100 * sites),
            compiler_params=room(8),
            name="combine",
        )(*operands)

    step = depth - 1
    seen = across(block, step)
    pair = pair[0]
    pair_back = across(pair, 0)
    seen_back = across(seen, 0)

    here, side = pl.pallas_call(
        functools.partial(edge_kernel, planes, half, step),
        out_shape=(shape(24 * half + max(raw_rows, 8), LANES), shape(24 * half, LANES)),
        in_specs=in_vmem(5),
        out_specs=tuple(in_vmem(2)),
        cost_estimate=cost(20 * sites, 10 * sites),
        compiler_params=room(8),
        name="edge",
    )(block, prefix, pair, seen, raw)
    here = lax.ppermute(here, "gx", [(i, (i - 1) % parts_gx) for i in range(parts_gx)])
    side = lax.ppermute(
        side, ("ta", "gx"),
        [(i * parts_gx + j, (i ^ 1) * parts_gx + (j - 1) % parts_gx)
         for i in range(times_ta) for j in range(parts_gx)],
    )

    def results(count):
        return [(count, slices, 18, planes, LANES), (count, slices, planes, LANES)]

    early, late = len(jobs_of(half, False)), len(jobs_of(half, True))
    field_shape = (half, 18 * (slices + 1), planes, LANES)
    field, out, trace = pl.pallas_call(
        functools.partial(early_kernel, planes, half, step),
        out_shape=tuple(shape(*s) for s in [field_shape] + results(early)),
        in_specs=in_vmem(4),
        out_specs=tuple(in_vmem(3)),
        cost_estimate=cost(2000 * sites, 400 * sites),
        compiler_params=room(8),
        name="early",
    )(links, block, prefix, seen)
    edge_shape = (18 * (slices + 1) * half, LANES)
    return pl.pallas_call(
        functools.partial(late_kernel, planes, half, step),
        out_shape=(shape(slices, 3, 18, planes, cells), shape(slices, 3, planes, cells)),
        in_specs=in_vmem(8),
        out_specs=tuple(anywhere(2)),
        scratch_shapes=[pltpu.VMEM(s, f32) for s in [field_shape, edge_shape, edge_shape] + results(late)]
        + [pltpu.SemaphoreType.DMA((early, 2)), pltpu.SemaphoreType.DMA((late, 2))],
        cost_estimate=cost(2500 * sites, 600 * sites),
        compiler_params=room(12),
        name="late",
    )(links, pair_back, seen_back, here, side, field, out, trace)


def solution(mesh):
    in_specs = (P("ta", None, None, "gx", None),)
    out_specs = (P("ta", None, None, "gx", None), P("ta", None, "gx", None))
    return jax.shard_map(on_device, mesh=mesh, in_specs=in_specs, out_specs=out_specs, check_vma=False)
```

time: 30.7 us -> 27.8 us (0.906)
  the two profiles are of different devices: /device:TPU:0 before, /device:TPU:25 now
where the time goes in v1:
time: 27.8 us; the launch traced here: 27.7 us
  waiting for transfers between devices  12.7 us (46%)
  starting transfers between devices  8.74 us (31%)
  Pallas kernels  4.3 us (15%)
  local copies, waits for them, and re-layouts  1.26 us (5%)
  between operations  0.67 us (2%)
    ppermute x5, waiting for transfers between devices, across(): return lax.ppermute(x, 'ta', [(i, i ^ 1 << step) for i in range(times_ta)])  9.57 us
    ppermute x1, starting transfers between devices, on_device(): lax.ppermute(here, 'gx', [(i, (i - 1) % parts_gx) for i in range(parts_gx)])  4.46 us
    ppermute x5, starting transfers between devices, across(): return lax.ppermute(x, 'ta', [(i, i ^ 1 << step) for i in range(times_ta)])  4.08 us
    ppermute x1, waiting for transfers between devices, on_device(): lax.ppermute(side, ('ta', 'gx'), [(i * parts_gx + j, (i ^ 1) * parts_gx +...  3.15 us
    pallas_call x1, Pallas kernels, on_device(): pl.pallas_call(functools.partial(late_kernel, planes, half, step), out_sh...  3.03 us
    squeeze x1, local copies, waits for them, and re-layouts, on_device(): links[:, 3]  1.26 us
    pallas_call x1, Pallas kernels, on_device(): pl.pallas_call(functools.partial(early_kernel, planes, half, step), out_s...  0.79 us
  transfers between devices with their start and end apart: 7, of which 4 were waited for; matrix products, arithmetic and copies ran while one was open for 0% of the time, Pallas kernels for 3%

profile of v1, /device:TPU:25, one launch (start us, length us, event | category | flops | bytes accessed | tf_op | source)
XLA Modules:
  0.0 27.7 jit_solution(8551280596626125842)
XLA Ops:
  0.6 0.0 copy-start
  0.6 1.3 %slice_bitcast_fusion.links_ref = f32[2,18,8,512]{3,2,1,0:T(8,128)S(1)} fusion(f32[2,4,18,8,512]{4,3,2,1,0:T(8,128)} %links_ref.3), kind=kLoop, calls=%fused_computation | loop fusion | bytes 1179648 | tf_op jit(solution)/shard_map/squeeze | solution.py:355
  1.9 0.1 block_product.1
  2.0 1.3 %collective-permute-start = (f32[192,128]{1,0:T(8,128)S(1)}, f32[192,128]{1,0:T(8,128)S(1)}, u32[]{:S(2)}, u32[]{:S(2)}) collective-permute-start(f32[192,128]{1,0:T(8,128)S(1)} %get-tuple-element.16), channel_id=1, source_target_pairs={{0,4},{4,0},{8,12},{12,8},{16,20},{20,16},{24,28},{28,24},{1,5},{5... | collective-permute-start | bytes 294920 | tf_op jit(solution)/shard_map/ppermute | solution.py:345
  3.3 2.3 %collective-permute-done.seen_ref = f32[192,128]{1,0:T(8,128)S(1)} collective-permute-done((f32[192,128]{1,0:T(8,128)S(1)}, f32[192,128]{1,0:T(8,128)S(1)}, u32[]{:S(2)}, u32[]{:S(2)}) %collective-permute-start) | collective-permute-done | bytes 98336 | tf_op jit(solution)/shard_map/ppermute | solution.py:345
  5.6 0.1 pair.1
  5.6 0.2 collective-permute-start.1
  5.9 3.3 %collective-permute-done.1.refs_1_ = f32[192,128]{1,0:T(8,128)S(1)} collective-permute-done((f32[192,128]{1,0:T(8,128)S(1)}, f32[192,128]{1,0:T(8,128)S(1)}, u32[]{:S(2)}, u32[]{:S(2)}) %collective-permute-start.1) | collective-permute-done | bytes 98336 | tf_op jit(solution)/shard_map/ppermute | solution.py:345
  9.2 0.1 combine.1
  9.3 0.1 collective-permute-start.3
  9.4 1.2 %collective-permute-start.2 = (f32[384,128]{1,0:T(8,128)S(1)}, f32[384,128]{1,0:T(8,128)S(1)}, u32[]{:S(2)}, u32[]{:S(2)}) collective-permute-start(f32[384,128]{1,0:T(8,128)S(1)} %get-tuple-element.19.pair_ref), channel_id=1, source_target_pairs={{0,4},{4,0},{8,12},{12,8},{16,20},{20,16},{24,28},{28,24},{1,5},{5... | collective-permute-start | bytes 589832 | tf_op jit(solution)/shard_map/ppermute | solution.py:345
  10.6 4.0 %collective-permute-done.3.seen_ref = f32[192,128]{1,0:T(8,128)S(1)} collective-permute-done((f32[192,128]{1,0:T(8,128)S(1)}, f32[192,128]{1,0:T(8,128)S(1)}, u32[]{:S(2)}, u32[]{:S(2)}) %collective-permute-start.3) | collective-permute-done | bytes 98336 | tf_op jit(solution)/shard_map/ppermute | solution.py:345
  14.7 1.2 %collective-permute-start.4 = (f32[192,128]{1,0:T(8,128)S(1)}, f32[192,128]{1,0:T(8,128)S(1)}, u32[]{:S(2)}, u32[]{:S(2)}) collective-permute-start(f32[192,128]{1,0:T(8,128)S(1)} %collective-permute-done.3.seen_ref), channel_id=1, source_target_pairs={{0,4},{4,0},{8,12},{12,8},{16,20},{20,16},{24,28},{28,24},{1,5},{5... | collective-permute-start | bytes 294920 | tf_op jit(solution)/shard_map/ppermute | solution.py:345
  15.9 0.2 edge.1
  16.0 4.5 %collective-permute-start.5 = (f32[96,128]{1,0:T(8,128)S(1)}, f32[96,128]{1,0:T(8,128)S(1)}, u32[]{:S(2)}, u32[]{:S(2)}) collective-permute-start(f32[96,128]{1,0:T(8,128)S(1)} %get-tuple-element.23), channel_id=1, source_target_pairs={{0,3},{1,0},{2,1},{3,2},{4,7},{5,4},{6,5},{7,6},{8,11},{9,8},{10,9... | collective-permute-start | bytes 147464 | tf_op jit(solution)/shard_map/ppermute | solution.py:399
  20.5 0.2 collective-permute-start.6
  20.7 0.0 copy-done
  20.7 0.8 %early.1 = (f32[2,54,8,128]{3,2,1,0:T(8,128)S(1)}, f32[3,2,18,8,128]{4,3,2,1,0:T(8,128)S(1)}, f32[3,2,8,128]{3,2,1,0:T(8,128)S(1)}) custom-call(f32[2,4,18,8,512]{4,3,2,1,0:T(8,128)S(1)} %copy-done, f32[192,128]{1,0:T(8,128)S(1)} %get-tuple-element.20.block_ref, f32[192,128]{1,0:T(8,128)S(1)} %get-tuple-element.21.prefix_ref, ...), custom_call_target="tpu_custom_call" | custom-call | flops 8192000 | bytes 1638400 | tf_op jit(solution)/shard_map/early/pallas_call | solution.py:411
  21.5 3.1 %collective-permute-done.6.side_ref = f32[48,128]{1,0:T(8,128)S(1)} collective-permute-done((f32[48,128]{1,0:T(8,128)S(1)}, f32[48,128]{1,0:T(8,128)S(1)}, u32[]{:S(2)}, u32[]{:S(2)}) %collective-permute-start.6) | collective-permute-done | bytes 24608 | tf_op jit(solution)/shard_map/ppermute | solution.py:400
  24.6 0.0 collective-permute-done.5.here_ref
  24.6 0.0 collective-permute-done.4.seen_ref
  24.7 0.0 collective-permute-done.2.pair_ref
  24.7 3.0 %late.1 = (f32[2,3,18,8,512]{4,3,2,1,0:T(8,128)}, f32[2,3,8,512]{3,2,1,0:T(8,128)}) custom-call(f32[2,4,18,8,512]{4,3,2,1,0:T(8,128)S(1)} %copy-done, f32[384,128]{1,0:T(8,128)S(1)} %collective-permute-done.2.pair_ref, f32[192,128]{1,0:T(8,128)S(1)} %collective-permute-done.4.seen_ref, f32[96,128]{1,0:T(8,128)S(1)} %collective-permute-done.5.here_ref, ...), custom_call_target="tpu_custom_call" | custom-call | flops 10240000 | bytes 2457600 | tf_op jit(solution)/shard_map/late/pallas_call | solution.py:421
Async XLA Ops:
  0.6 20.1 %copy-start = (f32[2,4,18,8,512]{4,3,2,1,0:T(8,128)S(1)}, f32[2,4,18,8,512]{4,3,2,1,0:T(8,128)}, u32[]{:S(2)}) copy-start(f32[2,4,18,8,512]{4,3,2,1,0:T(8,128)} %links_ref.3) | copy-start | bytes 7077892
  2.0 3.5 %collective-permute-start = (f32[192,128]{1,0:T(8,128)S(1)}, f32[192,128]{1,0:T(8,128)S(1)}, u32[]{:S(2)}, u32[]{:S(2)}) collective-permute-start(f32[192,128]{1,0:T(8,128)S(1)} %get-tuple-element.16), channel_id=1, source_target_pairs={{0,4},{4,0},{8,12},{12,8},{16,20},{20,16},{24,28},{28,24},{1,5},{5... | collective-permute-start | bytes 294920 | tf_op jit(solution)/shard_map/ppermute | solution.py:345
  5.6 3.5 %collective-permute-start.1 = (f32[192,128]{1,0:T(8,128)S(1)}, f32[192,128]{1,0:T(8,128)S(1)}, u32[]{:S(2)}, u32[]{:S(2)}) collective-permute-start(f32[192,128]{1,0:T(8,128)S(1)} %get-tuple-element.17.refs_0_), channel_id=1, source_target_pairs={{0,8},{4,12},{8,0},{12,4},{16,24},{20,28},{24,16},{28,20},{1,9},{5... | collective-permute-start | bytes 294920 | tf_op jit(solution)/shard_map/ppermute | solution.py:345
  9.3 5.4 %collective-permute-start.3 = (f32[192,128]{1,0:T(8,128)S(1)}, f32[192,128]{1,0:T(8,128)S(1)}, u32[]{:S(2)}, u32[]{:S(2)}) collective-permute-start(f32[192,128]{1,0:T(8,128)S(1)} %get-tuple-element.20.block_ref), channel_id=1, source_target_pairs={{0,16},{4,20},{8,24},{12,28},{16,0},{20,4},{24,8},{28,12},{1,17},{... | collective-permute-start | bytes 294920 | tf_op jit(solution)/shard_map/ppermute | solution.py:345
  9.4 15.2 %collective-permute-start.2 = (f32[384,128]{1,0:T(8,128)S(1)}, f32[384,128]{1,0:T(8,128)S(1)}, u32[]{:S(2)}, u32[]{:S(2)}) collective-permute-start(f32[384,128]{1,0:T(8,128)S(1)} %get-tuple-element.19.pair_ref), channel_id=1, source_target_pairs={{0,4},{4,0},{8,12},{12,8},{16,20},{20,16},{24,28},{28,24},{1,5},{5... | collective-permute-start | bytes 589832 | tf_op jit(solution)/shard_map/ppermute | solution.py:345
  14.7 10.0 %collective-permute-start.4 = (f32[192,128]{1,0:T(8,128)S(1)}, f32[192,128]{1,0:T(8,128)S(1)}, u32[]{:S(2)}, u32[]{:S(2)}) collective-permute-start(f32[192,128]{1,0:T(8,128)S(1)} %collective-permute-done.3.seen_ref), channel_id=1, source_target_pairs={{0,4},{4,0},{8,12},{12,8},{16,20},{20,16},{24,28},{28,24},{1,5},{5... | collective-permute-start | bytes 294920 | tf_op jit(solution)/shard_map/ppermute | solution.py:345
  16.0 8.6 %collective-permute-start.5 = (f32[96,128]{1,0:T(8,128)S(1)}, f32[96,128]{1,0:T(8,128)S(1)}, u32[]{:S(2)}, u32[]{:S(2)}) collective-permute-start(f32[96,128]{1,0:T(8,128)S(1)} %get-tuple-element.23), channel_id=1, source_target_pairs={{0,3},{1,0},{2,1},{3,2},{4,7},{5,4},{6,5},{7,6},{8,11},{9,8},{10,9... | collective-permute-start | bytes 147464 | tf_op jit(solution)/shard_map/ppermute | solution.py:399
  20.5 4.2 %collective-permute-start.6 = (f32[48,128]{1,0:T(8,128)S(1)}, f32[48,128]{1,0:T(8,128)S(1)}, u32[]{:S(2)}, u32[]{:S(2)}) collective-permute-start(f32[48,128]{1,0:T(8,128)S(1)} %get-tuple-element.24), channel_id=1, source_target_pairs={{0,7},{1,4},{2,5},{3,6},{4,3},{5,0},{6,1},{7,2},{8,15},{9,12},{10,... | collective-permute-start | bytes 73736 | tf_op jit(solution)/shard_map/ppermute | solution.py:400

commit v2 on v1

--- a/solution.py
+++ b/solution.py
@@ -270,44 +270,51 @@
     )
 
 
-def jobs_of(half, late):
+def jobs_of(half, stage):
     early = [(r, 2) for r in range(half)] + [(r, 1) for r in range(half - 1)]
-    rest = [(r, d) for r in range(2 * half) for d in range(3) if (r, d) not in early]
-    return rest if late else early
+    late = [(half - 1, 1)] + [(r, d) for r in range(half, 2 * half) for d in (1, 2)]
+    return (early, late, [(r, 0) for r in range(2 * half)])[stage]
 
 
 def early_kernel(planes, half, step, links_ref, block_ref, prefix_ref, seen_ref, field_ref, out_ref, trace_ref):
     prepare(planes, half, step, False, links_ref, lambda g: take(block_ref, g),
             lambda g: take(prefix_ref, g), lambda g: take(seen_ref, g), field_ref)
-    outputs(half, jobs_of(half, False), links_ref, [field_ref, field_ref], None, out_ref, trace_ref, lambda job: None)
-
-
-def late_kernel(planes, half, step, links_ref, pair_ref, seen_ref, here_ref, side_ref, field_ref, out_early,
-                trace_early, spatial_ref, correlator_ref, field_late, edge_own, edge_late, out_ref, trace_ref,
-                sem_early, sem):
-    slices, blocks = links_ref.shape[0], links_ref.shape[-1] // LANES
-    first = functools.partial(copies, half, jobs_of(half, False), out_early, trace_early,
-                              spatial_ref, correlator_ref, sem_early)
-    second = functools.partial(copies, half, jobs_of(half, True), out_ref, trace_ref,
-                               spatial_ref, correlator_ref, sem)
-    for job in range(len(jobs_of(half, False))):
-        for copy in first(job):
-            copy.start()
+    outputs(half, jobs_of(half, 0), links_ref, [field_ref, field_ref], None, out_ref, trace_ref, lambda job: None)
+
+
+def late_kernel(planes, half, step, links_ref, pair_ref, seen_ref, field_own, field_ref, out_ref, trace_ref):
     size = 12 * half * planes
     prepare(planes, half, step, True, links_ref, lambda g: take(pair_ref, g),
-            lambda g: take(pair_ref, g, size), lambda g: take(seen_ref, g), field_late)
+            lambda g: take(pair_ref, g, size), lambda g: take(seen_ref, g), field_ref)
+    outputs(half, jobs_of(half, 1), links_ref, [field_own, field_ref], None, out_ref, trace_ref, lambda job: None)
+
+
+def last_kernel(half, links_ref, here_ref, side_ref, field_own, field_other, out_early, trace_early,
+                out_late, trace_late, spatial_ref, correlator_ref, edge_own, edge_other, out_ref, trace_ref,
+                sem_early, sem_late, sem):
+    slices, blocks = links_ref.shape[0], links_ref.shape[-1] // LANES
+    made = []
+    for stage, refs in enumerate(((out_early, trace_early, sem_early), (out_late, trace_late, sem_late),
+                                  (out_ref, trace_ref, sem))):
+        out, trace, flags = refs
+        jobs = jobs_of(half, stage)
+        made.append([copies(half, jobs, out, trace, spatial_ref, correlator_ref, flags, j) for j in range(len(jobs))])
+    for pairs in made[:2]:
+        for pair in pairs:
+            for copy in pair:
+                copy.start()
     prepare_edge(half, slices, blocks, False, here_ref, here_ref, edge_own)
-    prepare_edge(half, slices, blocks, True, side_ref, here_ref, edge_late)
+    prepare_edge(half, slices, blocks, True, side_ref, here_ref, edge_other)
 
     def done(job):
-        for copy in second(job):
+        for copy in made[2][job]:
             copy.start()
 
-    outputs(half, jobs_of(half, True), links_ref, [field_ref, field_late], [edge_own, edge_late],
+    outputs(half, jobs_of(half, 2), links_ref, [field_own, field_other], [edge_own, edge_other],
             out_ref, trace_ref, done)
-    for count, make in ((len(jobs_of(half, False)), first), (len(jobs_of(half, True)), second)):
-        for job in range(count):
-            for copy in make(job):
+    for pairs in made:
+        for pair in pairs:
+            for copy in pair:
                 copy.wait()
 
 
@@ -406,29 +413,38 @@
     def results(count):
         return [(count, slices, 18, planes, LANES), (count, slices, planes, LANES)]
 
-    early, late = len(jobs_of(half, False)), len(jobs_of(half, True))
+    counts = [len(jobs_of(half, stage)) for stage in range(3)]
     field_shape = (half, 18 * (slices + 1), planes, LANES)
-    field, out, trace = pl.pallas_call(
+    field_own, out_early, trace_early = pl.pallas_call(
         functools.partial(early_kernel, planes, half, step),
-        out_shape=tuple(shape(*s) for s in [field_shape] + results(early)),
+        out_shape=tuple(shape(*s) for s in [field_shape] + results(counts[0])),
         in_specs=in_vmem(4),
         out_specs=tuple(in_vmem(3)),
-        cost_estimate=cost(2000 * sites, 400 * sites),
+        cost_estimate=cost(1200 * sites, 400 * sites),
         compiler_params=room(8),
         name="early",
     )(links, block, prefix, seen)
+    field_other, out_late, trace_late = pl.pallas_call(
+        functools.partial(late_kernel, planes, half, step),
+        out_shape=tuple(shape(*s) for s in [field_shape] + results(counts[1])),
+        in_specs=in_vmem(4),
+        out_specs=tuple(in_vmem(3)),
+        cost_estimate=cost(2000 * sites, 600 * sites),
+        compiler_params=room(8),
+        name="late",
+    )(links, pair_back, seen_back, field_own)
     edge_shape = (18 * (slices + 1) * half, LANES)
     return pl.pallas_call(
-        functools.partial(late_kernel, planes, half, step),
+        functools.partial(last_kernel, half),
         out_shape=(shape(slices, 3, 18, planes, cells), shape(slices, 3, planes, cells)),
-        in_specs=in_vmem(8),
+        in_specs=in_vmem(9),
         out_specs=tuple(anywhere(2)),
-        scratch_shapes=[pltpu.VMEM(s, f32) for s in [field_shape, edge_shape, edge_shape] + results(late)]
-        + [pltpu.SemaphoreType.DMA((early, 2)), pltpu.SemaphoreType.DMA((late, 2))],
-        cost_estimate=cost(2500 * sites, 600 * sites),
+        scratch_shapes=[pltpu.VMEM(s, f32) for s in [edge_shape, edge_shape] + results(counts[2])]
+        + [pltpu.SemaphoreType.DMA((count, 2)) for count in counts],
+        cost_estimate=cost(1500 * sites, 600 * sites),
         compiler_params=room(12),
-        name="late",
-    )(links, pair_back, seen_back, here, side, field, out, trace)
+        name="last",
+    )(links, here, side, field_own, field_other, out_early, trace_early, out_late, trace_late)
 
 
 def solution(mesh):

time: 27.8 us -> 26.6 us (0.957)
  the two profiles are of different devices: /device:TPU:25 before, /device:TPU:0 now
where the time goes in v2:
time: 26.6 us; the launch traced here: 26.2 us
  starting transfers between devices  13 us (49%)
  waiting for transfers between devices  6.94 us (26%)
  Pallas kernels  4.34 us (16%)
  local copies, waits for them, and re-layouts  1.26 us (5%)
  between operations  0.69 us (3%)
    ppermute x5, starting transfers between devices, across(): return lax.ppermute(x, 'ta', [(i, i ^ 1 << step) for i in range(times_ta)])  11.3 us
    ppermute x5, waiting for transfers between devices, across(): return lax.ppermute(x, 'ta', [(i, i ^ 1 << step) for i in range(times_ta)])  6.94 us
    pallas_call x1, Pallas kernels, on_device(): pl.pallas_call(functools.partial(last_kernel, half), out_shape=(shape(sli...  1.85 us
    ppermute x1, starting transfers between devices, on_device(): lax.ppermute(side, ('ta', 'gx'), [(i * parts_gx + j, (i ^ 1) * parts_gx +...  1.59 us
    squeeze x1, local copies, waits for them, and re-layouts, on_device(): links[:, 3]  1.26 us
    pallas_call x1, Pallas kernels, on_device(): pl.pallas_call(functools.partial(late_kernel, planes, half, step), out_sh...  1.19 us
    pallas_call x1, Pallas kernels, on_device(): pl.pallas_call(functools.partial(early_kernel, planes, half, step), out_s...  0.83 us
  transfers between devices with their start and end apart: 7, of which 4 were waited for; matrix products, arithmetic and copies ran while one was open for 0% of the time, Pallas kernels for 8%

profile of v2, /device:TPU:0, one launch (start us, length us, event | category | flops | bytes accessed | tf_op | source)
XLA Modules:
  0.0 26.2 jit_solution(16339549793423437390)
XLA Ops:
  0.6 0.0 copy-start
  0.6 1.3 %slice_bitcast_fusion.links_ref = f32[2,18,8,512]{3,2,1,0:T(8,128)S(1)} fusion(f32[2,4,18,8,512]{4,3,2,1,0:T(8,128)} %links_ref.5), kind=kLoop, calls=%fused_computation | loop fusion | bytes 1179648 | tf_op jit(solution)/shard_map/squeeze | solution.py:362
  1.9 0.1 block_product.1
  2.0 3.0 %collective-permute-start = (f32[192,128]{1,0:T(8,128)S(1)}, f32[192,128]{1,0:T(8,128)S(1)}, u32[]{:S(2)}, u32[]{:S(2)}) collective-permute-start(f32[192,128]{1,0:T(8,128)S(1)} %get-tuple-element.19), channel_id=1, source_target_pairs={{0,4},{4,0},{8,12},{12,8},{16,20},{20,16},{24,28},{28,24},{1,5},{5... | collective-permute-start | bytes 294920 | tf_op jit(solution)/shard_map/ppermute | solution.py:352
  5.1 2.8 %collective-permute-done.seen_ref = f32[192,128]{1,0:T(8,128)S(1)} collective-permute-done((f32[192,128]{1,0:T(8,128)S(1)}, f32[192,128]{1,0:T(8,128)S(1)}, u32[]{:S(2)}, u32[]{:S(2)}) %collective-permute-start) | collective-permute-done | bytes 98336 | tf_op jit(solution)/shard_map/ppermute | solution.py:352
  7.8 0.1 pair.1
  7.9 2.0 %collective-permute-start.1 = (f32[192,128]{1,0:T(8,128)S(1)}, f32[192,128]{1,0:T(8,128)S(1)}, u32[]{:S(2)}, u32[]{:S(2)}) collective-permute-start(f32[192,128]{1,0:T(8,128)S(1)} %get-tuple-element.20.refs_0_), channel_id=1, source_target_pairs={{0,8},{4,12},{8,0},{12,4},{16,24},{20,28},{24,16},{28,20},{1,9},{5... | collective-permute-start | bytes 294920 | tf_op jit(solution)/shard_map/ppermute | solution.py:352
  9.9 2.7 %collective-permute-done.1.refs_1_ = f32[192,128]{1,0:T(8,128)S(1)} collective-permute-done((f32[192,128]{1,0:T(8,128)S(1)}, f32[192,128]{1,0:T(8,128)S(1)}, u32[]{:S(2)}, u32[]{:S(2)}) %collective-permute-start.1) | collective-permute-done | bytes 98336 | tf_op jit(solution)/shard_map/ppermute | solution.py:352
  12.6 0.1 combine.1
  12.7 3.0 %collective-permute-start.2 = (f32[192,128]{1,0:T(8,128)S(1)}, f32[192,128]{1,0:T(8,128)S(1)}, u32[]{:S(2)}, u32[]{:S(2)}) collective-permute-start(f32[192,128]{1,0:T(8,128)S(1)} %get-tuple-element.22.block_ref), channel_id=1, source_target_pairs={{0,16},{4,20},{8,24},{12,28},{16,0},{20,4},{24,8},{28,12},{1,17},{... | collective-permute-start | bytes 294920 | tf_op jit(solution)/shard_map/ppermute | solution.py:352
  15.7 1.5 %collective-permute-start.5 = (f32[384,128]{1,0:T(8,128)S(1)}, f32[384,128]{1,0:T(8,128)S(1)}, u32[]{:S(2)}, u32[]{:S(2)}) collective-permute-start(f32[384,128]{1,0:T(8,128)S(1)} %get-tuple-element.24.pair_ref), channel_id=1, source_target_pairs={{0,4},{4,0},{8,12},{12,8},{16,20},{20,16},{24,28},{28,24},{1,5},{5... | collective-permute-start | bytes 589832 | tf_op jit(solution)/shard_map/ppermute | solution.py:352
  17.2 1.1 %collective-permute-done.2.seen_ref = f32[192,128]{1,0:T(8,128)S(1)} collective-permute-done((f32[192,128]{1,0:T(8,128)S(1)}, f32[192,128]{1,0:T(8,128)S(1)}, u32[]{:S(2)}, u32[]{:S(2)}) %collective-permute-start.2) | collective-permute-done | bytes 98336 | tf_op jit(solution)/shard_map/ppermute | solution.py:352
  18.3 1.8 %collective-permute-start.6 = (f32[192,128]{1,0:T(8,128)S(1)}, f32[192,128]{1,0:T(8,128)S(1)}, u32[]{:S(2)}, u32[]{:S(2)}) collective-permute-start(f32[192,128]{1,0:T(8,128)S(1)} %collective-permute-done.2.seen_ref), channel_id=1, source_target_pairs={{0,4},{4,0},{8,12},{12,8},{16,20},{20,16},{24,28},{28,24},{1,5},{5... | collective-permute-start | bytes 294920 | tf_op jit(solution)/shard_map/ppermute | solution.py:352
  20.1 0.2 edge.1
  20.3 0.1 collective-permute-start.3
  20.4 1.6 %collective-permute-start.4 = (f32[48,128]{1,0:T(8,128)S(1)}, f32[48,128]{1,0:T(8,128)S(1)}, u32[]{:S(2)}, u32[]{:S(2)}) collective-permute-start(f32[48,128]{1,0:T(8,128)S(1)} %get-tuple-element.27), channel_id=1, source_target_pairs={{0,7},{1,4},{2,5},{3,6},{4,3},{5,0},{6,1},{7,2},{8,15},{9,12},{10,... | collective-permute-start | bytes 73736 | tf_op jit(solution)/shard_map/ppermute | solution.py:407
  22.0 0.0 copy-done
  22.0 0.8 %early.1 = (f32[2,54,8,128]{3,2,1,0:T(8,128)S(1)}, f32[3,2,18,8,128]{4,3,2,1,0:T(8,128)S(1)}, f32[3,2,8,128]{3,2,1,0:T(8,128)S(1)}) custom-call(f32[2,4,18,8,512]{4,3,2,1,0:T(8,128)S(1)} %copy-done, f32[192,128]{1,0:T(8,128)S(1)} %get-tuple-element.22.block_ref, f32[192,128]{1,0:T(8,128)S(1)} %get-tuple-element.23.prefix_ref, ...), custom_call_target="tpu_custom_call" | custom-call | flops 4915200 | bytes 1638400 | tf_op jit(solution)/shard_map/early/pallas_call | solution.py:418
  22.8 0.3 %collective-permute-done.6.seen_ref = f32[192,128]{1,0:T(8,128)S(1)} collective-permute-done((f32[192,128]{1,0:T(8,128)S(1)}, f32[192,128]{1,0:T(8,128)S(1)}, u32[]{:S(2)}, u32[]{:S(2)}) %collective-permute-start.6) | collective-permute-done | bytes 98336 | tf_op jit(solution)/shard_map/ppermute | solution.py:352
  23.1 0.0 collective-permute-done.5.pair_ref
  23.1 1.2 %late.1 = (f32[2,54,8,128]{3,2,1,0:T(8,128)S(1)}, f32[5,2,18,8,128]{4,3,2,1,0:T(8,128)S(1)}, f32[5,2,8,128]{3,2,1,0:T(8,128)S(1)}) custom-call(f32[2,4,18,8,512]{4,3,2,1,0:T(8,128)S(1)} %copy-done, f32[384,128]{1,0:T(8,128)S(1)} %collective-permute-done.5.pair_ref, f32[192,128]{1,0:T(8,128)S(1)} %collective-permute-done.6.seen_ref, ...), custom_call_target="tpu_custom_call" | custom-call | flops 8192000 | bytes 2457600 | tf_op jit(solution)/shard_map/late/pallas_call | solution.py:427
  24.3 0.0 collective-permute-done.4.side_ref
  24.3 0.0 collective-permute-done.3.here_ref
  24.4 1.8 %last.1 = (f32[2,3,18,8,512]{4,3,2,1,0:T(8,128)}, f32[2,3,8,512]{3,2,1,0:T(8,128)}) custom-call(f32[2,4,18,8,512]{4,3,2,1,0:T(8,128)S(1)} %copy-done, f32[96,128]{1,0:T(8,128)S(1)} %collective-permute-done.3.here_ref, f32[48,128]{1,0:T(8,128)S(1)} %collective-permute-done.4.side_ref, f32[2,54,8,128]{3,2,1,0:T(8,128)S(1)} %get-tuple-element.28.field_own, ...), custom_call_target="tpu_custom_call" | custom-call | flops 6144000 | bytes 2457600 | tf_op jit(solution)/shard_map/last/pallas_call | solution.py:437
Async XLA Ops:
  0.6 21.3 %copy-start = (f32[2,4,18,8,512]{4,3,2,1,0:T(8,128)S(1)}, f32[2,4,18,8,512]{4,3,2,1,0:T(8,128)}, u32[]{:S(2)}) copy-start(f32[2,4,18,8,512]{4,3,2,1,0:T(8,128)} %links_ref.5) | copy-start | bytes 7077892
  2.0 5.8 %collective-permute-start = (f32[192,128]{1,0:T(8,128)S(1)}, f32[192,128]{1,0:T(8,128)S(1)}, u32[]{:S(2)}, u32[]{:S(2)}) collective-permute-start(f32[192,128]{1,0:T(8,128)S(1)} %get-tuple-element.19), channel_id=1, source_target_pairs={{0,4},{4,0},{8,12},{12,8},{16,20},{20,16},{24,28},{28,24},{1,5},{5... | collective-permute-start | bytes 294920 | tf_op jit(solution)/shard_map/ppermute | solution.py:352
  7.9 4.7 %collective-permute-start.1 = (f32[192,128]{1,0:T(8,128)S(1)}, f32[192,128]{1,0:T(8,128)S(1)}, u32[]{:S(2)}, u32[]{:S(2)}) collective-permute-start(f32[192,128]{1,0:T(8,128)S(1)} %get-tuple-element.20.refs_0_), channel_id=1, source_target_pairs={{0,8},{4,12},{8,0},{12,4},{16,24},{20,28},{24,16},{28,20},{1,9},{5... | collective-permute-start | bytes 294920 | tf_op jit(solution)/shard_map/ppermute | solution.py:352
  12.7 5.6 %collective-permute-start.2 = (f32[192,128]{1,0:T(8,128)S(1)}, f32[192,128]{1,0:T(8,128)S(1)}, u32[]{:S(2)}, u32[]{:S(2)}) collective-permute-start(f32[192,128]{1,0:T(8,128)S(1)} %get-tuple-element.22.block_ref), channel_id=1, source_target_pairs={{0,16},{4,20},{8,24},{12,28},{16,0},{20,4},{24,8},{28,12},{1,17},{... | collective-permute-start | bytes 294920 | tf_op jit(solution)/shard_map/ppermute | solution.py:352
  15.7 7.4 %collective-permute-start.5 = (f32[384,128]{1,0:T(8,128)S(1)}, f32[384,128]{1,0:T(8,128)S(1)}, u32[]{:S(2)}, u32[]{:S(2)}) collective-permute-start(f32[384,128]{1,0:T(8,128)S(1)} %get-tuple-element.24.pair_ref), channel_id=1, source_target_pairs={{0,4},{4,0},{8,12},{12,8},{16,20},{20,16},{24,28},{28,24},{1,5},{5... | collective-permute-start | bytes 589832 | tf_op jit(solution)/shard_map/ppermute | solution.py:352
  18.3 4.8 %collective-permute-start.6 = (f32[192,128]{1,0:T(8,128)S(1)}, f32[192,128]{1,0:T(8,128)S(1)}, u32[]{:S(2)}, u32[]{:S(2)}) collective-permute-start(f32[192,128]{1,0:T(8,128)S(1)} %collective-permute-done.2.seen_ref), channel_id=1, source_target_pairs={{0,4},{4,0},{8,12},{12,8},{16,20},{20,16},{24,28},{28,24},{1,5},{5... | collective-permute-start | bytes 294920 | tf_op jit(solution)/shard_map/ppermute | solution.py:352
  20.3 4.0 %collective-permute-start.3 = (f32[96,128]{1,0:T(8,128)S(1)}, f32[96,128]{1,0:T(8,128)S(1)}, u32[]{:S(2)}, u32[]{:S(2)}) collective-permute-start(f32[96,128]{1,0:T(8,128)S(1)} %get-tuple-element.26), channel_id=1, source_target_pairs={{0,3},{1,0},{2,1},{3,2},{4,7},{5,4},{6,5},{7,6},{8,11},{9,8},{10,9... | collective-permute-start | bytes 147464 | tf_op jit(solution)/shard_map/ppermute | solution.py:406
  20.4 4.0 %collective-permute-start.4 = (f32[48,128]{1,0:T(8,128)S(1)}, f32[48,128]{1,0:T(8,128)S(1)}, u32[]{:S(2)}, u32[]{:S(2)}) collective-permute-start(f32[48,128]{1,0:T(8,128)S(1)} %get-tuple-element.27), channel_id=1, source_target_pairs={{0,7},{1,4},{2,5},{3,6},{4,3},{5,0},{6,1},{7,2},{8,15},{9,12},{10,... | collective-permute-start | bytes 73736 | tf_op jit(solution)/shard_map/ppermute | solution.py:407

commit v3 on v2

--- a/solution.py
+++ b/solution.py
@@ -6,6 +6,7 @@
 from jax.experimental import pallas as pl
 from jax.experimental.pallas import tpu as pltpu
 from jax.sharding import PartitionSpec as P
+
 
 LZ = 32
 LANES = 128
@@ -98,6 +99,7 @@
 def give(ref, rows, matrix, base=0):
     def at(k, value):
         ref[pl.ds(rows(k).start + base, rows(k).size), :] = value
+
     put(at, matrix)
 
 
@@ -109,7 +111,10 @@
     return pl.ds(pl.multiple_of(c * LANES, LANES), LANES)
 
 
-def block_kernel(half, links_ref, keep_ref, send_ref, raw_ref):
+def block_kernel(half, whole_ref, keep_ref, send_ref, raw_ref, links_ref, sem):
+    copy = pltpu.make_async_copy(whole_ref.at[:, 3], links_ref, sem)
+    copy.start()
+    copy.wait()
     slices, _, planes, cells = links_ref.shape
     blocks = cells // LANES
     own = bit_of(0)
@@ -122,6 +127,7 @@
             for t in range(1, slices):
                 def edge(k, value):
                     raw_ref[pl.ds((12 * (t - 1) + k) * blocks + c, 1), :] = value
+
                 put(edge, [[(v[0][:1], v[1][:1]) for v in row] for row in link(t - 1)[:2]])
                 rows = times(rows, link(t))
             give(keep_ref if which == 0 else send_ref, groups(planes, half)[block], rows)
@@ -190,8 +196,10 @@
         for t in range(slices + 1):
             if 0 < t < slices:
                 gauge = times(gauge, matrix_at(lambda k: links_ref[t - 1, 3, k, :, at], 3))
+
             def store(k, v):
                 field_ref[local, 18 * t + k] = v
+
             put(store, complete(gauge if t < slices else poly))
 
 
@@ -206,8 +214,10 @@
             base = 2 * rows_of + 12 * blocks * (t - 1)
             link = matrix_at(lambda k: raw_ref[pl.ds(base + k * blocks + start, half), :], 2)
             gauge = times(gauge, complete(link))
+
         def store(k, v):
             out_ref[pl.ds((18 * t + k) * half, half), :] = v
+
         put(store, complete(gauge if t < slices else poly))
 
 
@@ -245,6 +255,7 @@
         def neighbour(base):
             def one(k):
                 return shifted(lambda q: field(q, base + k), direction, r, lambda q: edge(q, base + k))
+
             return matrix_at(one, 3)
 
         poly = matrix_at(lambda k: field(r, 18 * slices + k), 3)
@@ -253,8 +264,10 @@
             link = matrix_at(lambda k: links_ref[t, direction, k, :, at], 3)
             gauge = matrix_at(lambda k: field(r, 18 * t + k), 3)[:2]
             moved = complete(times_dagger(times(gauge, link), neighbour(18 * t)))
+
             def store(k, v):
                 out_ref[job, t, k] = v
+
             put(store, moved)
             around = complete(times_dagger(times_dagger(moved[:2], poly_next), moved))
             trace_ref[job, t] = trace_of_product(poly, around)
@@ -354,12 +367,13 @@
     keep, send, raw = pl.pallas_call(
         functools.partial(block_kernel, half),
         out_shape=(shape(size, LANES), shape(size, LANES), shape(max(raw_rows, 8), LANES)),
-        in_specs=in_vmem(1),
+        in_specs=anywhere(1),
         out_specs=tuple(in_vmem(3)),
+        scratch_shapes=[pltpu.VMEM((slices, 18, planes, cells), f32), pltpu.SemaphoreType.DMA],
         cost_estimate=cost(200 * sites, 90 * sites),
         compiler_params=room(8),
         name="block_product",
-    )(links[:, 3])
+    )(pltpu.with_memory_space_constraint(links, pltpu.HBM))
 
     seen = across(send, 0)
     block, lower = pl.pallas_call(

time: 26.6 us -> 26.6 us (level)
  local copies, waits for them, and re-layouts: 1.26 us -> 0.01 us
  Pallas kernels: 4.34 us -> 5.55 us
    squeeze x1 -> x0, local copies, waits for them, and re-layouts: 1.26 us -> none  [on_device(): links[:, 3]]
    pallas_call x1, Pallas kernels: 0.12 us -> 1.33 us  [on_device(): pl.pallas_call(functools.partial(block_kernel, half), out_shape=(shape(si...]
where the time goes in v3:
time: 26.6 us; the launch traced here: 26.2 us
  starting transfers between devices  13 us (49%)
  waiting for transfers between devices  6.95 us (26%)
  Pallas kernels  5.55 us (21%)
  between operations  0.69 us (3%)
    ppermute x5, starting transfers between devices, across(): return lax.ppermute(x, 'ta', [(i, i ^ 1 << step) for i in range(times_ta)])  11.3 us
    ppermute x5, waiting for transfers between devices, across(): return lax.ppermute(x, 'ta', [(i, i ^ 1 << step) for i in range(times_ta)])  6.94 us
    pallas_call x1, Pallas kernels, on_device(): pl.pallas_call(functools.partial(last_kernel, half), out_shape=(shape(sli...  1.85 us
    ppermute x1, starting transfers between devices, on_device(): lax.ppermute(side, ('ta', 'gx'), [(i * parts_gx + j, (i ^ 1) * parts_gx +...  1.59 us
    pallas_call x1, Pallas kernels, on_device(): pl.pallas_call(functools.partial(block_kernel, half), out_shape=(shape(si...  1.33 us
    pallas_call x1, Pallas kernels, on_device(): pl.pallas_call(functools.partial(late_kernel, planes, half, step), out_sh...  1.2 us
    pallas_call x1, Pallas kernels, on_device(): pl.pallas_call(functools.partial(early_kernel, planes, half, step), out_s...  0.83 us
  transfers between devices with their start and end apart: 7, of which 4 were waited for; matrix products, arithmetic and copies ran while one was open for 0% of the time, Pallas kernels for 8%

profile of v3, /device:TPU:0, one launch (start us, length us, event | category | flops | bytes accessed | tf_op | source)
XLA Modules:
  0.0 26.2 jit_solution(14236992869350782988)
XLA Ops:
  0.6 0.0 copy-start
  0.6 1.3 %block_product.1 = (f32[192,128]{1,0:T(8,128)S(1)}, f32[192,128]{1,0:T(8,128)S(1)}, f32[48,128]{1,0:T(8,128)S(1)}) custom-call(f32[2,4,18,8,512]{4,3,2,1,0:T(8,128)} %links_ref.5), custom_call_target="tpu_custom_call" | custom-call | flops 819200 | bytes 368640 | tf_op jit(solution)/shard_map/block_product/pallas_call | solution.py:367
  2.0 3.0 %collective-permute-start = (f32[192,128]{1,0:T(8,128)S(1)}, f32[192,128]{1,0:T(8,128)S(1)}, u32[]{:S(2)}, u32[]{:S(2)}) collective-permute-start(f32[192,128]{1,0:T(8,128)S(1)} %get-tuple-element.19), channel_id=1, source_target_pairs={{0,4},{4,0},{8,12},{12,8},{16,20},{20,16},{24,28},{28,24},{1,5},{5... | collective-permute-start | bytes 294920 | tf_op jit(solution)/shard_map/ppermute | solution.py:365
  5.0 2.8 %collective-permute-done.seen_ref = f32[192,128]{1,0:T(8,128)S(1)} collective-permute-done((f32[192,128]{1,0:T(8,128)S(1)}, f32[192,128]{1,0:T(8,128)S(1)}, u32[]{:S(2)}, u32[]{:S(2)}) %collective-permute-start) | collective-permute-done | bytes 98336 | tf_op jit(solution)/shard_map/ppermute | solution.py:365
  7.8 0.1 pair.1
  7.9 2.0 %collective-permute-start.1 = (f32[192,128]{1,0:T(8,128)S(1)}, f32[192,128]{1,0:T(8,128)S(1)}, u32[]{:S(2)}, u32[]{:S(2)}) collective-permute-start(f32[192,128]{1,0:T(8,128)S(1)} %get-tuple-element.20.refs_0_), channel_id=1, source_target_pairs={{0,8},{4,12},{8,0},{12,4},{16,24},{20,28},{24,16},{28,20},{1,9},{5... | collective-permute-start | bytes 294920 | tf_op jit(solution)/shard_map/ppermute | solution.py:365
  9.8 2.7 %collective-permute-done.1.refs_1_ = f32[192,128]{1,0:T(8,128)S(1)} collective-permute-done((f32[192,128]{1,0:T(8,128)S(1)}, f32[192,128]{1,0:T(8,128)S(1)}, u32[]{:S(2)}, u32[]{:S(2)}) %collective-permute-start.1) | collective-permute-done | bytes 98336 | tf_op jit(solution)/shard_map/ppermute | solution.py:365
  12.5 0.1 combine.1
  12.7 3.0 %collective-permute-start.2 = (f32[192,128]{1,0:T(8,128)S(1)}, f32[192,128]{1,0:T(8,128)S(1)}, u32[]{:S(2)}, u32[]{:S(2)}) collective-permute-start(f32[192,128]{1,0:T(8,128)S(1)} %get-tuple-element.22.block_ref), channel_id=1, source_target_pairs={{0,16},{4,20},{8,24},{12,28},{16,0},{20,4},{24,8},{28,12},{1,17},{... | collective-permute-start | bytes 294920 | tf_op jit(solution)/shard_map/ppermute | solution.py:365
  15.7 1.5 %collective-permute-start.5 = (f32[384,128]{1,0:T(8,128)S(1)}, f32[384,128]{1,0:T(8,128)S(1)}, u32[]{:S(2)}, u32[]{:S(2)}) collective-permute-start(f32[384,128]{1,0:T(8,128)S(1)} %get-tuple-element.24.pair_ref), channel_id=1, source_target_pairs={{0,4},{4,0},{8,12},{12,8},{16,20},{20,16},{24,28},{28,24},{1,5},{5... | collective-permute-start | bytes 589832 | tf_op jit(solution)/shard_map/ppermute | solution.py:365
  17.2 1.1 %collective-permute-done.2.seen_ref = f32[192,128]{1,0:T(8,128)S(1)} collective-permute-done((f32[192,128]{1,0:T(8,128)S(1)}, f32[192,128]{1,0:T(8,128)S(1)}, u32[]{:S(2)}, u32[]{:S(2)}) %collective-permute-start.2) | collective-permute-done | bytes 98336 | tf_op jit(solution)/shard_map/ppermute | solution.py:365
  18.3 1.8 %collective-permute-start.6 = (f32[192,128]{1,0:T(8,128)S(1)}, f32[192,128]{1,0:T(8,128)S(1)}, u32[]{:S(2)}, u32[]{:S(2)}) collective-permute-start(f32[192,128]{1,0:T(8,128)S(1)} %collective-permute-done.2.seen_ref), channel_id=1, source_target_pairs={{0,4},{4,0},{8,12},{12,8},{16,20},{20,16},{24,28},{28,24},{1,5},{5... | collective-permute-start | bytes 294920 | tf_op jit(solution)/shard_map/ppermute | solution.py:365
  20.1 0.2 edge.1
  20.3 0.1 collective-permute-start.3
  20.3 1.6 %collective-permute-start.4 = (f32[48,128]{1,0:T(8,128)S(1)}, f32[48,128]{1,0:T(8,128)S(1)}, u32[]{:S(2)}, u32[]{:S(2)}) collective-permute-start(f32[48,128]{1,0:T(8,128)S(1)} %get-tuple-element.27), channel_id=1, source_target_pairs={{0,7},{1,4},{2,5},{3,6},{4,3},{5,0},{6,1},{7,2},{8,15},{9,12},{10,... | collective-permute-start | bytes 73736 | tf_op jit(solution)/shard_map/ppermute | solution.py:421
  21.9 0.0 copy-done
  21.9 0.8 %early.1 = (f32[2,54,8,128]{3,2,1,0:T(8,128)S(1)}, f32[3,2,18,8,128]{4,3,2,1,0:T(8,128)S(1)}, f32[3,2,8,128]{3,2,1,0:T(8,128)S(1)}) custom-call(f32[2,4,18,8,512]{4,3,2,1,0:T(8,128)S(1)} %copy-done, f32[192,128]{1,0:T(8,128)S(1)} %get-tuple-element.22.block_ref, f32[192,128]{1,0:T(8,128)S(1)} %get-tuple-element.23.prefix_ref, ...), custom_call_target="tpu_custom_call" | custom-call | flops 4915200 | bytes 1638400 | tf_op jit(solution)/shard_map/early/pallas_call | solution.py:432
  22.8 0.3 %collective-permute-done.6.seen_ref = f32[192,128]{1,0:T(8,128)S(1)} collective-permute-done((f32[192,128]{1,0:T(8,128)S(1)}, f32[192,128]{1,0:T(8,128)S(1)}, u32[]{:S(2)}, u32[]{:S(2)}) %collective-permute-start.6) | collective-permute-done | bytes 98336 | tf_op jit(solution)/shard_map/ppermute | solution.py:365
  23.1 0.0 collective-permute-done.5.pair_ref
  23.1 1.2 %late.1 = (f32[2,54,8,128]{3,2,1,0:T(8,128)S(1)}, f32[5,2,18,8,128]{4,3,2,1,0:T(8,128)S(1)}, f32[5,2,8,128]{3,2,1,0:T(8,128)S(1)}) custom-call(f32[2,4,18,8,512]{4,3,2,1,0:T(8,128)S(1)} %copy-done, f32[384,128]{1,0:T(8,128)S(1)} %collective-permute-done.5.pair_ref, f32[192,128]{1,0:T(8,128)S(1)} %collective-permute-done.6.seen_ref, ...), custom_call_target="tpu_custom_call" | custom-call | flops 8192000 | bytes 2457600 | tf_op jit(solution)/shard_map/late/pallas_call | solution.py:441
  24.3 0.0 collective-permute-done.4.side_ref
  24.3 0.0 collective-permute-done.3.here_ref
  24.3 1.8 %last.1 = (f32[2,3,18,8,512]{4,3,2,1,0:T(8,128)}, f32[2,3,8,512]{3,2,1,0:T(8,128)}) custom-call(f32[2,4,18,8,512]{4,3,2,1,0:T(8,128)S(1)} %copy-done, f32[96,128]{1,0:T(8,128)S(1)} %collective-permute-done.3.here_ref, f32[48,128]{1,0:T(8,128)S(1)} %collective-permute-done.4.side_ref, f32[2,54,8,128]{3,2,1,0:T(8,128)S(1)} %get-tuple-element.28.field_own, ...), custom_call_target="tpu_custom_call" | custom-call | flops 6144000 | bytes 2457600 | tf_op jit(solution)/shard_map/last/pallas_call | solution.py:451
Async XLA Ops:
  0.6 21.3 %copy-start = (f32[2,4,18,8,512]{4,3,2,1,0:T(8,128)S(1)}, f32[2,4,18,8,512]{4,3,2,1,0:T(8,128)}, u32[]{:S(2)}) copy-start(f32[2,4,18,8,512]{4,3,2,1,0:T(8,128)} %links_ref.5) | copy-start | bytes 7077892
  2.0 5.8 %collective-permute-start = (f32[192,128]{1,0:T(8,128)S(1)}, f32[192,128]{1,0:T(8,128)S(1)}, u32[]{:S(2)}, u32[]{:S(2)}) collective-permute-start(f32[192,128]{1,0:T(8,128)S(1)} %get-tuple-element.19), channel_id=1, source_target_pairs={{0,4},{4,0},{8,12},{12,8},{16,20},{20,16},{24,28},{28,24},{1,5},{5... | collective-permute-start | bytes 294920 | tf_op jit(solution)/shard_map/ppermute | solution.py:365
  7.9 4.7 %collective-permute-start.1 = (f32[192,128]{1,0:T(8,128)S(1)}, f32[192,128]{1,0:T(8,128)S(1)}, u32[]{:S(2)}, u32[]{:S(2)}) collective-permute-start(f32[192,128]{1,0:T(8,128)S(1)} %get-tuple-element.20.refs_0_), channel_id=1, source_target_pairs={{0,8},{4,12},{8,0},{12,4},{16,24},{20,28},{24,16},{28,20},{1,9},{5... | collective-permute-start | bytes 294920 | tf_op jit(solution)/shard_map/ppermute | solution.py:365
  12.7 5.6 %collective-permute-start.2 = (f32[192,128]{1,0:T(8,128)S(1)}, f32[192,128]{1,0:T(8,128)S(1)}, u32[]{:S(2)}, u32[]{:S(2)}) collective-permute-start(f32[192,128]{1,0:T(8,128)S(1)} %get-tuple-element.22.block_ref), channel_id=1, source_target_pairs={{0,16},{4,20},{8,24},{12,28},{16,0},{20,4},{24,8},{28,12},{1,17},{... | collective-permute-start | bytes 294920 | tf_op jit(solution)/shard_map/ppermute | solution.py:365
  15.7 7.4 %collective-permute-start.5 = (f32[384,128]{1,0:T(8,128)S(1)}, f32[384,128]{1,0:T(8,128)S(1)}, u32[]{:S(2)}, u32[]{:S(2)}) collective-permute-start(f32[384,128]{1,0:T(8,128)S(1)} %get-tuple-element.24.pair_ref), channel_id=1, source_target_pairs={{0,4},{4,0},{8,12},{12,8},{16,20},{20,16},{24,28},{28,24},{1,5},{5... | collective-permute-start | bytes 589832 | tf_op jit(solution)/shard_map/ppermute | solution.py:365
  18.3 4.8 %collective-permute-start.6 = (f32[192,128]{1,0:T(8,128)S(1)}, f32[192,128]{1,0:T(8,128)S(1)}, u32[]{:S(2)}, u32[]{:S(2)}) collective-permute-start(f32[192,128]{1,0:T(8,128)S(1)} %collective-permute-done.2.seen_ref), channel_id=1, source_target_pairs={{0,4},{4,0},{8,12},{12,8},{16,20},{20,16},{24,28},{28,24},{1,5},{5... | collective-permute-start | bytes 294920 | tf_op jit(solution)/shard_map/ppermute | solution.py:365
  20.3 4.0 %collective-permute-start.3 = (f32[96,128]{1,0:T(8,128)S(1)}, f32[96,128]{1,0:T(8,128)S(1)}, u32[]{:S(2)}, u32[]{:S(2)}) collective-permute-start(f32[96,128]{1,0:T(8,128)S(1)} %get-tuple-element.26), channel_id=1, source_target_pairs={{0,3},{1,0},{2,1},{3,2},{4,7},{5,4},{6,5},{7,6},{8,11},{9,8},{10,9... | collective-permute-start | bytes 147464 | tf_op jit(solution)/shard_map/ppermute | solution.py:420
  20.3 4.0 %collective-permute-start.4 = (f32[48,128]{1,0:T(8,128)S(1)}, f32[48,128]{1,0:T(8,128)S(1)}, u32[]{:S(2)}, u32[]{:S(2)}) collective-permute-start(f32[48,128]{1,0:T(8,128)S(1)} %get-tuple-element.27), channel_id=1, source_target_pairs={{0,7},{1,4},{2,5},{3,6},{4,3},{5,0},{6,1},{7,2},{8,15},{9,12},{10,... | collective-permute-start | bytes 73736 | tf_op jit(solution)/shard_map/ppermute | solution.py:421

commit v4 on v2

--- a/solution.py
+++ b/solution.py
@@ -7,6 +7,7 @@
 from jax.experimental.pallas import tpu as pltpu
 from jax.sharding import PartitionSpec as P
 
+
 LZ = 32
 LANES = 128
 
@@ -18,27 +19,37 @@
     return result
 
 
-def dot(left, right):
-    pairs = list(zip(left, right))
-    real = total([a[0] * b[0] for a, b in pairs]) - total([a[1] * b[1] for a, b in pairs])
-    imag = total([a[0] * b[1] for a, b in pairs] + [a[1] * b[0] for a, b in pairs])
-    return real, imag
-
-
-def dot_conj(left, right):
-    pairs = list(zip(left, right))
-    real = total([a[0] * b[0] for a, b in pairs] + [a[1] * b[1] for a, b in pairs])
-    imag = total([a[1] * b[0] for a, b in pairs]) - total([a[0] * b[1] for a, b in pairs])
-    return real, imag
+def real_dot(left, right):
+    return total([a * b for a, b in zip(left, right)])
+
+
+def triples(rows, sign):
+    return [([v[0] for v in row], [v[1] for v in row],
+             [v[0] + v[1] if sign > 0 else v[0] - v[1] for v in row]) for row in rows]
 
 
 def times(rows, matrix):
-    columns = [[matrix[k][j] for k in range(3)] for j in range(3)]
-    return [[dot(row, column) for column in columns] for row in rows]
+    columns = triples([[matrix[k][j] for k in range(3)] for j in range(3)], 1)
+    result = []
+    for left in triples(rows, 1):
+        line = []
+        for right in columns:
+            a, b, c = (real_dot(x, y) for x, y in zip(left, right))
+            line.append((a - b, c - a - b))
+        result.append(line)
+    return result
 
 
 def times_dagger(rows, matrix):
-    return [[dot_conj(row, other) for other in matrix] for row in rows]
+    others = triples(matrix, -1)
+    result = []
+    for left in triples(rows, 1):
+        line = []
+        for right in others:
+            a, b, c = (real_dot(x, y) for x, y in zip(left, right))
+            line.append((a + b, c - a + b))
+        result.append(line)
+    return result
 
 
 def complete(rows):
@@ -98,6 +109,7 @@
 def give(ref, rows, matrix, base=0):
     def at(k, value):
         ref[pl.ds(rows(k).start + base, rows(k).size), :] = value
+
     put(at, matrix)
 
 
@@ -109,22 +121,31 @@
     return pl.ds(pl.multiple_of(c * LANES, LANES), LANES)
 
 
-def block_kernel(half, links_ref, keep_ref, send_ref, raw_ref):
+def block_kernel(half, which, whole_ref, block_ref, *rest):
+    links_ref, sem = rest[-2:]
     slices, _, planes, cells = links_ref.shape
-    blocks = cells // LANES
+    blocks = whole_ref.shape[-1] // LANES
     own = bit_of(0)
-    for which in range(2):
-        for block in range(half):
-            c = (own if which == 0 else 1 - own) * half + block
-            at = lane_block(c)
-            link = lambda t: matrix_at(lambda k: links_ref[t, k, :, at], 3)
-            rows = link(0)[:2]
-            for t in range(1, slices):
+    start = (own if which == 0 else 1 - own) * half if which else 0
+    at = pl.ds(pl.multiple_of(start * LANES, LANES), cells)
+    copy = pltpu.make_async_copy(whole_ref.at[:, 3, :, :, at], links_ref, sem)
+    copy.start()
+    copy.wait()
+    for block in range(half):
+        at = lane_block(block if which else own * half + block)
+        link = lambda t: matrix_at(lambda k: links_ref[t, k, :, at], 3)
+        rows = link(0)[:2]
+        for t in range(1, slices):
+            rows = times(rows, link(t))
+        give(block_ref, groups(planes, half)[block], rows)
+    if which == 0:
+        for t in range(slices - 1):
+            for c in range(blocks):
                 def edge(k, value):
-                    raw_ref[pl.ds((12 * (t - 1) + k) * blocks + c, 1), :] = value
-                put(edge, [[(v[0][:1], v[1][:1]) for v in row] for row in link(t - 1)[:2]])
-                rows = times(rows, link(t))
-            give(keep_ref if which == 0 else send_ref, groups(planes, half)[block], rows)
+                    row = (12 * t + k) * blocks + c
+                    rest[0][row:row + 1, :] = value[:1]
+
+                put(edge, matrix_at(lambda k: links_ref[t, k, :, c * LANES:(c + 1) * LANES], 3)[:2])
 
 
 def pair_kernel(planes, half, keep_ref, seen_ref, block_ref, lower_ref):
@@ -190,8 +211,10 @@
         for t in range(slices + 1):
             if 0 < t < slices:
                 gauge = times(gauge, matrix_at(lambda k: links_ref[t - 1, 3, k, :, at], 3))
+
             def store(k, v):
                 field_ref[local, 18 * t + k] = v
+
             put(store, complete(gauge if t < slices else poly))
 
 
@@ -206,8 +229,10 @@
             base = 2 * rows_of + 12 * blocks * (t - 1)
             link = matrix_at(lambda k: raw_ref[pl.ds(base + k * blocks + start, half), :], 2)
             gauge = times(gauge, complete(link))
+
         def store(k, v):
             out_ref[pl.ds((18 * t + k) * half, half), :] = v
+
         put(store, complete(gauge if t < slices else poly))
 
 
@@ -245,6 +270,7 @@
         def neighbour(base):
             def one(k):
                 return shifted(lambda q: field(q, base + k), direction, r, lambda q: edge(q, base + k))
+
             return matrix_at(one, 3)
 
         poly = matrix_at(lambda k: field(r, 18 * slices + k), 3)
@@ -253,8 +279,10 @@
             link = matrix_at(lambda k: links_ref[t, direction, k, :, at], 3)
             gauge = matrix_at(lambda k: field(r, 18 * t + k), 3)[:2]
             moved = complete(times_dagger(times(gauge, link), neighbour(18 * t)))
+
             def store(k, v):
                 out_ref[job, t, k] = v
+
             put(store, moved)
             around = complete(times_dagger(times_dagger(moved[:2], poly_next), moved))
             trace_ref[job, t] = trace_of_product(poly, around)
@@ -351,17 +379,21 @@
     def across(x, step):
         return lax.ppermute(x, "ta", [(i, i ^ (1 << step)) for i in range(times_ta)])
 
-    keep, send, raw = pl.pallas_call(
-        functools.partial(block_kernel, half),
-        out_shape=(shape(size, LANES), shape(size, LANES), shape(max(raw_rows, 8), LANES)),
-        in_specs=in_vmem(1),
-        out_specs=tuple(in_vmem(3)),
-        cost_estimate=cost(200 * sites, 90 * sites),
-        compiler_params=room(8),
-        name="block_product",
-    )(links[:, 3])
-
+    def product(which, width, *more):
+        return pl.pallas_call(
+            functools.partial(block_kernel, half, which),
+            out_shape=(shape(size, LANES),) + more,
+            in_specs=anywhere(1),
+            out_specs=tuple(in_vmem(1 + len(more))),
+            scratch_shapes=[pltpu.VMEM((slices, 18, planes, width), f32), pltpu.SemaphoreType.DMA],
+            cost_estimate=cost(200 * sites, 90 * sites),
+            compiler_params=room(8),
+            name="block_product",
+        )(pltpu.with_memory_space_constraint(links, pltpu.HBM))
+
+    send, = product(1, half * LANES)
     seen = across(send, 0)
+    keep, raw = product(0, cells, shape(max(raw_rows, 8), LANES))
     block, lower = pl.pallas_call(
         functools.partial(pair_kernel, planes, half),
         out_shape=(shape(size, LANES), shape(size, LANES)),

time: 26.6 us -> 26.4 us (level)
  Pallas kernels: 4.34 us -> 6.42 us
  local copies, waits for them, and re-layouts: 1.26 us -> 0.01 us
  waiting for transfers between devices: 6.94 us -> 5.88 us
    pallas_call x1 -> x2, Pallas kernels: 0.12 us -> 2.3 us  [product(): pl.pallas_call(functools.partial(block_kernel, half, which), out_shape=(s...]
    squeeze x1 -> x0, local copies, waits for them, and re-layouts: 1.26 us -> none  [on_device(): links[:, 3]]
    ppermute x5, waiting for transfers between devices: 6.94 us -> 5.87 us  [across(): return lax.ppermute(x, 'ta', [(i, i ^ 1 << step) for i in range(times_ta)])]
  transfers between devices with their start and end apart: 7 -> 7, of which waited for: 4 -> 4; matrix products, arithmetic and copies ran while one was open for 0% -> 0% of each run, Pallas kernels for 8% -> 12%
where the time goes in v4:
time: 26.4 us; the launch traced here: 26 us
  starting transfers between devices  13 us (49%)
  Pallas kernels  6.42 us (24%)
  waiting for transfers between devices  5.88 us (22%)
  between operations  0.7 us (3%)
    ppermute x5, starting transfers between devices, across(): return lax.ppermute(x, 'ta', [(i, i ^ 1 << step) for i in range(times_ta)])  11.3 us
    ppermute x5, waiting for transfers between devices, across(): return lax.ppermute(x, 'ta', [(i, i ^ 1 << step) for i in range(times_ta)])  5.87 us
    pallas_call x2, Pallas kernels, product(): pl.pallas_call(functools.partial(block_kernel, half, which), out_shape=(s...  2.3 us
    pallas_call x1, Pallas kernels, on_device(): pl.pallas_call(functools.partial(last_kernel, half), out_shape=(shape(sli...  1.83 us
    ppermute x1, starting transfers between devices, on_device(): lax.ppermute(side, ('ta', 'gx'), [(i * parts_gx + j, (i ^ 1) * parts_gx +...  1.59 us
    pallas_call x1, Pallas kernels, on_device(): pl.pallas_call(functools.partial(late_kernel, planes, half, step), out_sh...  1.17 us
    pallas_call x1, Pallas kernels, on_device(): pl.pallas_call(functools.partial(early_kernel, planes, half, step), out_s...  0.78 us
  transfers between devices with their start and end apart: 7, of which 4 were waited for; matrix products, arithmetic and copies ran while one was open for 0% of the time, Pallas kernels for 12%

profile of v4, /device:TPU:0, one launch (start us, length us, event | category | flops | bytes accessed | tf_op | source)
XLA Modules:
  0.0 26.0 jit_solution(8437132673606955360)
XLA Ops:
  0.6 0.0 copy-start
  0.6 1.2 %block_product.3 = f32[192,128]{1,0:T(8,128)S(1)} custom-call(f32[2,4,18,8,512]{4,3,2,1,0:T(8,128)} %links_ref.5), custom_call_target="tpu_custom_call" | custom-call | flops 819200 | bytes 368640 | tf_op jit(solution)/shard_map/block_product/pallas_call | solution.py:383
  1.8 3.0 %collective-permute-start = (f32[192,128]{1,0:T(8,128)S(1)}, f32[192,128]{1,0:T(8,128)S(1)}, u32[]{:S(2)}, u32[]{:S(2)}) collective-permute-start(f32[192,128]{1,0:T(8,128)S(1)} %block_product.3), channel_id=1, source_target_pairs={{0,4},{4,0},{8,12},{12,8},{16,20},{20,16},{24,28},{28,24},{1,5},{5... | collective-permute-start | bytes 294920 | tf_op jit(solution)/shard_map/ppermute | solution.py:380
  4.9 1.1 %block_product.2 = (f32[192,128]{1,0:T(8,128)S(1)}, f32[48,128]{1,0:T(8,128)S(1)}) custom-call(f32[2,4,18,8,512]{4,3,2,1,0:T(8,128)} %links_ref.5), custom_call_target="tpu_custom_call" | custom-call | flops 819200 | bytes 368640 | tf_op jit(solution)/shard_map/block_product/pallas_call | solution.py:383
  6.0 1.7 %collective-permute-done.seen_ref = f32[192,128]{1,0:T(8,128)S(1)} collective-permute-done((f32[192,128]{1,0:T(8,128)S(1)}, f32[192,128]{1,0:T(8,128)S(1)}, u32[]{:S(2)}, u32[]{:S(2)}) %collective-permute-start) | collective-permute-done | bytes 98336 | tf_op jit(solution)/shard_map/ppermute | solution.py:380
  7.7 0.1 pair.1
  7.7 2.0 %collective-permute-start.1 = (f32[192,128]{1,0:T(8,128)S(1)}, f32[192,128]{1,0:T(8,128)S(1)}, u32[]{:S(2)}, u32[]{:S(2)}) collective-permute-start(f32[192,128]{1,0:T(8,128)S(1)} %get-tuple-element.18.refs_0_), channel_id=1, source_target_pairs={{0,8},{4,12},{8,0},{12,4},{16,24},{20,28},{24,16},{28,20},{1,9},{5... | collective-permute-start | bytes 294920 | tf_op jit(solution)/shard_map/ppermute | solution.py:380
  9.7 2.7 %collective-permute-done.1.refs_1_ = f32[192,128]{1,0:T(8,128)S(1)} collective-permute-done((f32[192,128]{1,0:T(8,128)S(1)}, f32[192,128]{1,0:T(8,128)S(1)}, u32[]{:S(2)}, u32[]{:S(2)}) %collective-permute-start.1) | collective-permute-done | bytes 98336 | tf_op jit(solution)/shard_map/ppermute | solution.py:380
  12.4 0.1 combine.1
  12.5 3.0 %collective-permute-start.2 = (f32[192,128]{1,0:T(8,128)S(1)}, f32[192,128]{1,0:T(8,128)S(1)}, u32[]{:S(2)}, u32[]{:S(2)}) collective-permute-start(f32[192,128]{1,0:T(8,128)S(1)} %get-tuple-element.20.block_ref), channel_id=1, source_target_pairs={{0,16},{4,20},{8,24},{12,28},{16,0},{20,4},{24,8},{28,12},{1,17},{... | collective-permute-start | bytes 294920 | tf_op jit(solution)/shard_map/ppermute | solution.py:380
  15.5 1.5 %collective-permute-start.5 = (f32[384,128]{1,0:T(8,128)S(1)}, f32[384,128]{1,0:T(8,128)S(1)}, u32[]{:S(2)}, u32[]{:S(2)}) collective-permute-start(f32[384,128]{1,0:T(8,128)S(1)} %get-tuple-element.22.pair_ref), channel_id=1, source_target_pairs={{0,4},{4,0},{8,12},{12,8},{16,20},{20,16},{24,28},{28,24},{1,5},{5... | collective-permute-start | bytes 589832 | tf_op jit(solution)/shard_map/ppermute | solution.py:380
  17.0 1.1 %collective-permute-done.2.seen_ref = f32[192,128]{1,0:T(8,128)S(1)} collective-permute-done((f32[192,128]{1,0:T(8,128)S(1)}, f32[192,128]{1,0:T(8,128)S(1)}, u32[]{:S(2)}, u32[]{:S(2)}) %collective-permute-start.2) | collective-permute-done | bytes 98336 | tf_op jit(solution)/shard_map/ppermute | solution.py:380
  18.1 1.8 %collective-permute-start.6 = (f32[192,128]{1,0:T(8,128)S(1)}, f32[192,128]{1,0:T(8,128)S(1)}, u32[]{:S(2)}, u32[]{:S(2)}) collective-permute-start(f32[192,128]{1,0:T(8,128)S(1)} %collective-permute-done.2.seen_ref), channel_id=1, source_target_pairs={{0,4},{4,0},{8,12},{12,8},{16,20},{20,16},{24,28},{28,24},{1,5},{5... | collective-permute-start | bytes 294920 | tf_op jit(solution)/shard_map/ppermute | solution.py:380
  19.9 0.2 edge.1
  20.1 0.1 collective-permute-start.3
  20.2 1.6 %collective-permute-start.4 = (f32[48,128]{1,0:T(8,128)S(1)}, f32[48,128]{1,0:T(8,128)S(1)}, u32[]{:S(2)}, u32[]{:S(2)}) collective-permute-start(f32[48,128]{1,0:T(8,128)S(1)} %get-tuple-element.25), channel_id=1, source_target_pairs={{0,7},{1,4},{2,5},{3,6},{4,3},{5,0},{6,1},{7,2},{8,15},{9,12},{10,... | collective-permute-start | bytes 73736 | tf_op jit(solution)/shard_map/ppermute | solution.py:439
  21.8 0.0 copy-done
  21.8 0.8 %early.1 = (f32[2,54,8,128]{3,2,1,0:T(8,128)S(1)}, f32[3,2,18,8,128]{4,3,2,1,0:T(8,128)S(1)}, f32[3,2,8,128]{3,2,1,0:T(8,128)S(1)}) custom-call(f32[2,4,18,8,512]{4,3,2,1,0:T(8,128)S(1)} %copy-done, f32[192,128]{1,0:T(8,128)S(1)} %get-tuple-element.20.block_ref, f32[192,128]{1,0:T(8,128)S(1)} %get-tuple-element.21.prefix_ref, ...), custom_call_target="tpu_custom_call" | custom-call | flops 4915200 | bytes 1638400 | tf_op jit(solution)/shard_map/early/pallas_call | solution.py:450
  22.5 0.4 %collective-permute-done.6.seen_ref = f32[192,128]{1,0:T(8,128)S(1)} collective-permute-done((f32[192,128]{1,0:T(8,128)S(1)}, f32[192,128]{1,0:T(8,128)S(1)}, u32[]{:S(2)}, u32[]{:S(2)}) %collective-permute-start.6) | collective-permute-done | bytes 98336 | tf_op jit(solution)/shard_map/ppermute | solution.py:380
  22.9 0.0 collective-permute-done.5.pair_ref
  22.9 1.2 %late.1 = (f32[2,54,8,128]{3,2,1,0:T(8,128)S(1)}, f32[5,2,18,8,128]{4,3,2,1,0:T(8,128)S(1)}, f32[5,2,8,128]{3,2,1,0:T(8,128)S(1)}) custom-call(f32[2,4,18,8,512]{4,3,2,1,0:T(8,128)S(1)} %copy-done, f32[384,128]{1,0:T(8,128)S(1)} %collective-permute-done.5.pair_ref, f32[192,128]{1,0:T(8,128)S(1)} %collective-permute-done.6.seen_ref, ...), custom_call_target="tpu_custom_call" | custom-call | flops 8192000 | bytes 2457600 | tf_op jit(solution)/shard_map/late/pallas_call | solution.py:459
  24.1 0.0 collective-permute-done.4.side_ref
  24.1 0.0 collective-permute-done.3.here_ref
  24.1 1.8 %last.1 = (f32[2,3,18,8,512]{4,3,2,1,0:T(8,128)}, f32[2,3,8,512]{3,2,1,0:T(8,128)}) custom-call(f32[2,4,18,8,512]{4,3,2,1,0:T(8,128)S(1)} %copy-done, f32[96,128]{1,0:T(8,128)S(1)} %collective-permute-done.3.here_ref, f32[48,128]{1,0:T(8,128)S(1)} %collective-permute-done.4.side_ref, f32[2,54,8,128]{3,2,1,0:T(8,128)S(1)} %get-tuple-element.26.field_own, ...), custom_call_target="tpu_custom_call" | custom-call | flops 6144000 | bytes 2457600 | tf_op jit(solution)/shard_map/last/pallas_call | solution.py:469
Async XLA Ops:
  0.6 21.1 %copy-start = (f32[2,4,18,8,512]{4,3,2,1,0:T(8,128)S(1)}, f32[2,4,18,8,512]{4,3,2,1,0:T(8,128)}, u32[]{:S(2)}) copy-start(f32[2,4,18,8,512]{4,3,2,1,0:T(8,128)} %links_ref.5) | copy-start | bytes 7077892
  1.8 5.8 %collective-permute-start = (f32[192,128]{1,0:T(8,128)S(1)}, f32[192,128]{1,0:T(8,128)S(1)}, u32[]{:S(2)}, u32[]{:S(2)}) collective-permute-start(f32[192,128]{1,0:T(8,128)S(1)} %block_product.3), channel_id=1, source_target_pairs={{0,4},{4,0},{8,12},{12,8},{16,20},{20,16},{24,28},{28,24},{1,5},{5... | collective-permute-start | bytes 294920 | tf_op jit(solution)/shard_map/ppermute | solution.py:380
  7.7 4.7 %collective-permute-start.1 = (f32[192,128]{1,0:T(8,128)S(1)}, f32[192,128]{1,0:T(8,128)S(1)}, u32[]{:S(2)}, u32[]{:S(2)}) collective-permute-start(f32[192,128]{1,0:T(8,128)S(1)} %get-tuple-element.18.refs_0_), channel_id=1, source_target_pairs={{0,8},{4,12},{8,0},{12,4},{16,24},{20,28},{24,16},{28,20},{1,9},{5... | collective-permute-start | bytes 294920 | tf_op jit(solution)/shard_map/ppermute | solution.py:380
  12.5 5.6 %collective-permute-start.2 = (f32[192,128]{1,0:T(8,128)S(1)}, f32[192,128]{1,0:T(8,128)S(1)}, u32[]{:S(2)}, u32[]{:S(2)}) collective-permute-start(f32[192,128]{1,0:T(8,128)S(1)} %get-tuple-element.20.block_ref), channel_id=1, source_target_pairs={{0,16},{4,20},{8,24},{12,28},{16,0},{20,4},{24,8},{28,12},{1,17},{... | collective-permute-start | bytes 294920 | tf_op jit(solution)/shard_map/ppermute | solution.py:380
  15.5 7.4 %collective-permute-start.5 = (f32[384,128]{1,0:T(8,128)S(1)}, f32[384,128]{1,0:T(8,128)S(1)}, u32[]{:S(2)}, u32[]{:S(2)}) collective-permute-start(f32[384,128]{1,0:T(8,128)S(1)} %get-tuple-element.22.pair_ref), channel_id=1, source_target_pairs={{0,4},{4,0},{8,12},{12,8},{16,20},{20,16},{24,28},{28,24},{1,5},{5... | collective-permute-start | bytes 589832 | tf_op jit(solution)/shard_map/ppermute | solution.py:380
  18.1 4.8 %collective-permute-start.6 = (f32[192,128]{1,0:T(8,128)S(1)}, f32[192,128]{1,0:T(8,128)S(1)}, u32[]{:S(2)}, u32[]{:S(2)}) collective-permute-start(f32[192,128]{1,0:T(8,128)S(1)} %collective-permute-done.2.seen_ref), channel_id=1, source_target_pairs={{0,4},{4,0},{8,12},{12,8},{16,20},{20,16},{24,28},{28,24},{1,5},{5... | collective-permute-start | bytes 294920 | tf_op jit(solution)/shard_map/ppermute | solution.py:380
  20.1 4.0 %collective-permute-start.3 = (f32[96,128]{1,0:T(8,128)S(1)}, f32[96,128]{1,0:T(8,128)S(1)}, u32[]{:S(2)}, u32[]{:S(2)}) collective-permute-start(f32[96,128]{1,0:T(8,128)S(1)} %get-tuple-element.24), channel_id=1, source_target_pairs={{0,3},{1,0},{2,1},{3,2},{4,7},{5,4},{6,5},{7,6},{8,11},{9,8},{10,9... | collective-permute-start | bytes 147464 | tf_op jit(solution)/shard_map/ppermute | solution.py:438
  20.2 3.9 %collective-permute-start.4 = (f32[48,128]{1,0:T(8,128)S(1)}, f32[48,128]{1,0:T(8,128)S(1)}, u32[]{:S(2)}, u32[]{:S(2)}) collective-permute-start(f32[48,128]{1,0:T(8,128)S(1)} %get-tuple-element.25), channel_id=1, source_target_pairs={{0,7},{1,4},{2,5},{3,6},{4,3},{5,0},{6,1},{7,2},{8,15},{9,12},{10,... | collective-permute-start | bytes 73736 | tf_op jit(solution)/shard_map/ppermute | solution.py:439

commit v5 on v4

--- a/solution.py
+++ b/solution.py
@@ -289,13 +289,8 @@
         done(job)
 
 
-def copies(half, jobs, out_ref, trace_ref, spatial_ref, correlator_ref, sem, job):
-    r, direction = jobs[job]
-    at = lane_block(lax.rem(bit_of(0) * half + r, 2 * half))
-    return (
-        pltpu.make_async_copy(out_ref.at[job], spatial_ref.at[:, direction, :, :, at], sem.at[job, 0]),
-        pltpu.make_async_copy(trace_ref.at[job], correlator_ref.at[:, direction, :, at], sem.at[job, 1]),
-    )
+def lanes_of(half, r):
+    return lane_block(lax.rem(bit_of(0) * half + r, 2 * half))
 
 
 def jobs_of(half, stage):
@@ -319,31 +314,36 @@
 
 def last_kernel(half, links_ref, here_ref, side_ref, field_own, field_other, out_early, trace_early,
                 out_late, trace_late, spatial_ref, correlator_ref, edge_own, edge_other, out_ref, trace_ref,
-                sem_early, sem_late, sem):
+                trace_all, sem_early, sem_late, sem, sem_all):
     slices, blocks = links_ref.shape[0], links_ref.shape[-1] // LANES
-    made = []
-    for stage, refs in enumerate(((out_early, trace_early, sem_early), (out_late, trace_late, sem_late),
-                                  (out_ref, trace_ref, sem))):
-        out, trace, flags = refs
-        jobs = jobs_of(half, stage)
-        made.append([copies(half, jobs, out, trace, spatial_ref, correlator_ref, flags, j) for j in range(len(jobs))])
-    for pairs in made[:2]:
-        for pair in pairs:
-            for copy in pair:
-                copy.start()
+    started = []
+
+    def write(out, flags, job, r, direction):
+        target = spatial_ref.at[:, direction, :, :, lanes_of(half, r)]
+        copy = pltpu.make_async_copy(out.at[job], target, flags.at[job])
+        copy.start()
+        started.append(copy)
+
+    def collect(trace, job, r, direction):
+        trace_all[:, direction, :, lanes_of(half, r)] = trace[job]
+
+    for stage, (out, trace, flags) in enumerate(((out_early, trace_early, sem_early), (out_late, trace_late, sem_late))):
+        for job, (r, direction) in enumerate(jobs_of(half, stage)):
+            write(out, flags, job, r, direction)
+            collect(trace, job, r, direction)
     prepare_edge(half, slices, blocks, False, here_ref, here_ref, edge_own)
     prepare_edge(half, slices, blocks, True, side_ref, here_ref, edge_other)
+    jobs = jobs_of(half, 2)
 
     def done(job):
-        for copy in made[2][job]:
-            copy.start()
-
-    outputs(half, jobs_of(half, 2), links_ref, [field_own, field_other], [edge_own, edge_other],
-            out_ref, trace_ref, done)
-    for pairs in made:
-        for pair in pairs:
-            for copy in pair:
-                copy.wait()
+        write(out_ref, sem, job, *jobs[job])
+        collect(trace_ref, job, *jobs[job])
+
+    outputs(half, jobs, links_ref, [field_own, field_other], [edge_own, edge_other], out_ref, trace_ref, done)
+    copy = pltpu.make_async_copy(trace_all, correlator_ref, sem_all)
+    copy.start()
+    for other in started + [copy]:
+        other.wait()
 
 
 def in_vmem(count):
@@ -472,7 +472,8 @@
         in_specs=in_vmem(9),
         out_specs=tuple(anywhere(2)),
         scratch_shapes=[pltpu.VMEM(s, f32) for s in [edge_shape, edge_shape] + results(counts[2])]
-        + [pltpu.SemaphoreType.DMA((count, 2)) for count in counts],
+        + [pltpu.VMEM((slices, 3, planes, cells), f32)]
+        + [pltpu.SemaphoreType.DMA((count,)) for count in counts] + [pltpu.SemaphoreType.DMA],
         cost_estimate=cost(1500 * sites, 600 * sites),
         compiler_params=room(12),
         name="last",

time: 26.4 us -> 26.3 us (level)
  no operation moved by 1% of the time
where the time goes in v5:
time: 26.3 us; the launch traced here: 25.8 us
  starting transfers between devices  13 us (49%)
  Pallas kernels  6.27 us (24%)
  waiting for transfers between devices  5.88 us (22%)
  between operations  0.7 us (3%)
    ppermute x5, starting transfers between devices, across(): return lax.ppermute(x, 'ta', [(i, i ^ 1 << step) for i in range(times_ta)])  11.3 us
    ppermute x5, waiting for transfers between devices, across(): return lax.ppermute(x, 'ta', [(i, i ^ 1 << step) for i in range(times_ta)])  5.87 us
    pallas_call x2, Pallas kernels, product(): pl.pallas_call(functools.partial(block_kernel, half, which), out_shape=(s...  2.3 us
    pallas_call x1, Pallas kernels, on_device(): pl.pallas_call(functools.partial(last_kernel, half), out_shape=(shape(sli...  1.69 us
    ppermute x1, starting transfers between devices, on_device(): lax.ppermute(side, ('ta', 'gx'), [(i * parts_gx + j, (i ^ 1) * parts_gx +...  1.59 us
    pallas_call x1, Pallas kernels, on_device(): pl.pallas_call(functools.partial(late_kernel, planes, half, step), out_sh...  1.17 us
    pallas_call x1, Pallas kernels, on_device(): pl.pallas_call(functools.partial(early_kernel, planes, half, step), out_s...  0.78 us
  transfers between devices with their start and end apart: 7, of which 4 were waited for; matrix products, arithmetic and copies ran while one was open for 0% of the time, Pallas kernels for 12%

profile of v5, /device:TPU:0, one launch (start us, length us, event | category | flops | bytes accessed | tf_op | source)
XLA Modules:
  0.0 25.8 jit_solution(14849329967860243357)
XLA Ops:
  0.6 0.0 copy-start
  0.6 1.2 %block_product.3 = f32[192,128]{1,0:T(8,128)S(1)} custom-call(f32[2,4,18,8,512]{4,3,2,1,0:T(8,128)} %links_ref.5), custom_call_target="tpu_custom_call" | custom-call | flops 819200 | bytes 368640 | tf_op jit(solution)/shard_map/block_product/pallas_call | solution.py:383
  1.8 3.0 %collective-permute-start = (f32[192,128]{1,0:T(8,128)S(1)}, f32[192,128]{1,0:T(8,128)S(1)}, u32[]{:S(2)}, u32[]{:S(2)}) collective-permute-start(f32[192,128]{1,0:T(8,128)S(1)} %block_product.3), channel_id=1, source_target_pairs={{0,4},{4,0},{8,12},{12,8},{16,20},{20,16},{24,28},{28,24},{1,5},{5... | collective-permute-start | bytes 294920 | tf_op jit(solution)/shard_map/ppermute | solution.py:380
  4.9 1.1 %block_product.2 = (f32[192,128]{1,0:T(8,128)S(1)}, f32[48,128]{1,0:T(8,128)S(1)}) custom-call(f32[2,4,18,8,512]{4,3,2,1,0:T(8,128)} %links_ref.5), custom_call_target="tpu_custom_call" | custom-call | flops 819200 | bytes 368640 | tf_op jit(solution)/shard_map/block_product/pallas_call | solution.py:383
  6.0 1.7 %collective-permute-done.seen_ref = f32[192,128]{1,0:T(8,128)S(1)} collective-permute-done((f32[192,128]{1,0:T(8,128)S(1)}, f32[192,128]{1,0:T(8,128)S(1)}, u32[]{:S(2)}, u32[]{:S(2)}) %collective-permute-start) | collective-permute-done | bytes 98336 | tf_op jit(solution)/shard_map/ppermute | solution.py:380
  7.7 0.1 pair.1
  7.7 2.0 %collective-permute-start.1 = (f32[192,128]{1,0:T(8,128)S(1)}, f32[192,128]{1,0:T(8,128)S(1)}, u32[]{:S(2)}, u32[]{:S(2)}) collective-permute-start(f32[192,128]{1,0:T(8,128)S(1)} %get-tuple-element.18.refs_0_), channel_id=1, source_target_pairs={{0,8},{4,12},{8,0},{12,4},{16,24},{20,28},{24,16},{28,20},{1,9},{5... | collective-permute-start | bytes 294920 | tf_op jit(solution)/shard_map/ppermute | solution.py:380
  9.7 2.7 %collective-permute-done.1.refs_1_ = f32[192,128]{1,0:T(8,128)S(1)} collective-permute-done((f32[192,128]{1,0:T(8,128)S(1)}, f32[192,128]{1,0:T(8,128)S(1)}, u32[]{:S(2)}, u32[]{:S(2)}) %collective-permute-start.1) | collective-permute-done | bytes 98336 | tf_op jit(solution)/shard_map/ppermute | solution.py:380
  12.4 0.1 combine.1
  12.5 3.0 %collective-permute-start.2 = (f32[192,128]{1,0:T(8,128)S(1)}, f32[192,128]{1,0:T(8,128)S(1)}, u32[]{:S(2)}, u32[]{:S(2)}) collective-permute-start(f32[192,128]{1,0:T(8,128)S(1)} %get-tuple-element.20.block_ref), channel_id=1, source_target_pairs={{0,16},{4,20},{8,24},{12,28},{16,0},{20,4},{24,8},{28,12},{1,17},{... | collective-permute-start | bytes 294920 | tf_op jit(solution)/shard_map/ppermute | solution.py:380
  15.5 1.5 %collective-permute-start.5 = (f32[384,128]{1,0:T(8,128)S(1)}, f32[384,128]{1,0:T(8,128)S(1)}, u32[]{:S(2)}, u32[]{:S(2)}) collective-permute-start(f32[384,128]{1,0:T(8,128)S(1)} %get-tuple-element.22.pair_ref), channel_id=1, source_target_pairs={{0,4},{4,0},{8,12},{12,8},{16,20},{20,16},{24,28},{28,24},{1,5},{5... | collective-permute-start | bytes 589832 | tf_op jit(solution)/shard_map/ppermute | solution.py:380
  17.0 1.1 %collective-permute-done.2.seen_ref = f32[192,128]{1,0:T(8,128)S(1)} collective-permute-done((f32[192,128]{1,0:T(8,128)S(1)}, f32[192,128]{1,0:T(8,128)S(1)}, u32[]{:S(2)}, u32[]{:S(2)}) %collective-permute-start.2) | collective-permute-done | bytes 98336 | tf_op jit(solution)/shard_map/ppermute | solution.py:380
  18.1 1.8 %collective-permute-start.6 = (f32[192,128]{1,0:T(8,128)S(1)}, f32[192,128]{1,0:T(8,128)S(1)}, u32[]{:S(2)}, u32[]{:S(2)}) collective-permute-start(f32[192,128]{1,0:T(8,128)S(1)} %collective-permute-done.2.seen_ref), channel_id=1, source_target_pairs={{0,4},{4,0},{8,12},{12,8},{16,20},{20,16},{24,28},{28,24},{1,5},{5... | collective-permute-start | bytes 294920 | tf_op jit(solution)/shard_map/ppermute | solution.py:380
  19.9 0.2 edge.1
  20.1 0.1 collective-permute-start.3
  20.2 1.6 %collective-permute-start.4 = (f32[48,128]{1,0:T(8,128)S(1)}, f32[48,128]{1,0:T(8,128)S(1)}, u32[]{:S(2)}, u32[]{:S(2)}) collective-permute-start(f32[48,128]{1,0:T(8,128)S(1)} %get-tuple-element.25), channel_id=1, source_target_pairs={{0,7},{1,4},{2,5},{3,6},{4,3},{5,0},{6,1},{7,2},{8,15},{9,12},{10,... | collective-permute-start | bytes 73736 | tf_op jit(solution)/shard_map/ppermute | solution.py:439
  21.8 0.0 copy-done
  21.8 0.8 %early.1 = (f32[2,54,8,128]{3,2,1,0:T(8,128)S(1)}, f32[3,2,18,8,128]{4,3,2,1,0:T(8,128)S(1)}, f32[3,2,8,128]{3,2,1,0:T(8,128)S(1)}) custom-call(f32[2,4,18,8,512]{4,3,2,1,0:T(8,128)S(1)} %copy-done, f32[192,128]{1,0:T(8,128)S(1)} %get-tuple-element.20.block_ref, f32[192,128]{1,0:T(8,128)S(1)} %get-tuple-element.21.prefix_ref, ...), custom_call_target="tpu_custom_call" | custom-call | flops 4915200 | bytes 1638400 | tf_op jit(solution)/shard_map/early/pallas_call | solution.py:450
  22.5 0.4 %collective-permute-done.6.seen_ref = f32[192,128]{1,0:T(8,128)S(1)} collective-permute-done((f32[192,128]{1,0:T(8,128)S(1)}, f32[192,128]{1,0:T(8,128)S(1)}, u32[]{:S(2)}, u32[]{:S(2)}) %collective-permute-start.6) | collective-permute-done | bytes 98336 | tf_op jit(solution)/shard_map/ppermute | solution.py:380
  22.9 0.0 collective-permute-done.5.pair_ref
  22.9 1.2 %late.1 = (f32[2,54,8,128]{3,2,1,0:T(8,128)S(1)}, f32[5,2,18,8,128]{4,3,2,1,0:T(8,128)S(1)}, f32[5,2,8,128]{3,2,1,0:T(8,128)S(1)}) custom-call(f32[2,4,18,8,512]{4,3,2,1,0:T(8,128)S(1)} %copy-done, f32[384,128]{1,0:T(8,128)S(1)} %collective-permute-done.5.pair_ref, f32[192,128]{1,0:T(8,128)S(1)} %collective-permute-done.6.seen_ref, ...), custom_call_target="tpu_custom_call" | custom-call | flops 8192000 | bytes 2457600 | tf_op jit(solution)/shard_map/late/pallas_call | solution.py:459
  24.1 0.0 collective-permute-done.4.side_ref
  24.1 0.0 collective-permute-done.3.here_ref
  24.1 1.7 %last.1 = (f32[2,3,18,8,512]{4,3,2,1,0:T(8,128)}, f32[2,3,8,512]{3,2,1,0:T(8,128)}) custom-call(f32[2,4,18,8,512]{4,3,2,1,0:T(8,128)S(1)} %copy-done, f32[96,128]{1,0:T(8,128)S(1)} %collective-permute-done.3.here_ref, f32[48,128]{1,0:T(8,128)S(1)} %collective-permute-done.4.side_ref, f32[2,54,8,128]{3,2,1,0:T(8,128)S(1)} %get-tuple-element.26.field_own, ...), custom_call_target="tpu_custom_call" | custom-call | flops 6144000 | bytes 2457600 | tf_op jit(solution)/shard_map/last/pallas_call | solution.py:469
Async XLA Ops:
  0.6 21.1 %copy-start = (f32[2,4,18,8,512]{4,3,2,1,0:T(8,128)S(1)}, f32[2,4,18,8,512]{4,3,2,1,0:T(8,128)}, u32[]{:S(2)}) copy-start(f32[2,4,18,8,512]{4,3,2,1,0:T(8,128)} %links_ref.5) | copy-start | bytes 7077892
  1.8 5.8 %collective-permute-start = (f32[192,128]{1,0:T(8,128)S(1)}, f32[192,128]{1,0:T(8,128)S(1)}, u32[]{:S(2)}, u32[]{:S(2)}) collective-permute-start(f32[192,128]{1,0:T(8,128)S(1)} %block_product.3), channel_id=1, source_target_pairs={{0,4},{4,0},{8,12},{12,8},{16,20},{20,16},{24,28},{28,24},{1,5},{5... | collective-permute-start | bytes 294920 | tf_op jit(solution)/shard_map/ppermute | solution.py:380
  7.7 4.7 %collective-permute-start.1 = (f32[192,128]{1,0:T(8,128)S(1)}, f32[192,128]{1,0:T(8,128)S(1)}, u32[]{:S(2)}, u32[]{:S(2)}) collective-permute-start(f32[192,128]{1,0:T(8,128)S(1)} %get-tuple-element.18.refs_0_), channel_id=1, source_target_pairs={{0,8},{4,12},{8,0},{12,4},{16,24},{20,28},{24,16},{28,20},{1,9},{5... | collective-permute-start | bytes 294920 | tf_op jit(solution)/shard_map/ppermute | solution.py:380
  12.5 5.6 %collective-permute-start.2 = (f32[192,128]{1,0:T(8,128)S(1)}, f32[192,128]{1,0:T(8,128)S(1)}, u32[]{:S(2)}, u32[]{:S(2)}) collective-permute-start(f32[192,128]{1,0:T(8,128)S(1)} %get-tuple-element.20.block_ref), channel_id=1, source_target_pairs={{0,16},{4,20},{8,24},{12,28},{16,0},{20,4},{24,8},{28,12},{1,17},{... | collective-permute-start | bytes 294920 | tf_op jit(solution)/shard_map/ppermute | solution.py:380
  15.5 7.4 %collective-permute-start.5 = (f32[384,128]{1,0:T(8,128)S(1)}, f32[384,128]{1,0:T(8,128)S(1)}, u32[]{:S(2)}, u32[]{:S(2)}) collective-permute-start(f32[384,128]{1,0:T(8,128)S(1)} %get-tuple-element.22.pair_ref), channel_id=1, source_target_pairs={{0,4},{4,0},{8,12},{12,8},{16,20},{20,16},{24,28},{28,24},{1,5},{5... | collective-permute-start | bytes 589832 | tf_op jit(solution)/shard_map/ppermute | solution.py:380
  18.1 4.8 %collective-permute-start.6 = (f32[192,128]{1,0:T(8,128)S(1)}, f32[192,128]{1,0:T(8,128)S(1)}, u32[]{:S(2)}, u32[]{:S(2)}) collective-permute-start(f32[192,128]{1,0:T(8,128)S(1)} %collective-permute-done.2.seen_ref), channel_id=1, source_target_pairs={{0,4},{4,0},{8,12},{12,8},{16,20},{20,16},{24,28},{28,24},{1,5},{5... | collective-permute-start | bytes 294920 | tf_op jit(solution)/shard_map/ppermute | solution.py:380
  20.1 4.0 %collective-permute-start.3 = (f32[96,128]{1,0:T(8,128)S(1)}, f32[96,128]{1,0:T(8,128)S(1)}, u32[]{:S(2)}, u32[]{:S(2)}) collective-permute-start(f32[96,128]{1,0:T(8,128)S(1)} %get-tuple-element.24), channel_id=1, source_target_pairs={{0,3},{1,0},{2,1},{3,2},{4,7},{5,4},{6,5},{7,6},{8,11},{9,8},{10,9... | collective-permute-start | bytes 147464 | tf_op jit(solution)/shard_map/ppermute | solution.py:438
  20.2 3.9 %collective-permute-start.4 = (f32[48,128]{1,0:T(8,128)S(1)}, f32[48,128]{1,0:T(8,128)S(1)}, u32[]{:S(2)}, u32[]{:S(2)}) collective-permute-start(f32[48,128]{1,0:T(8,128)S(1)} %get-tuple-element.25), channel_id=1, source_target_pairs={{0,7},{1,4},{2,5},{3,6},{4,3},{5,0},{6,1},{7,2},{8,15},{9,12},{10,... | collective-permute-start | bytes 73736 | tf_op jit(solution)/shard_map/ppermute | solution.py:439

commit v6 on v5

--- a/solution.py
+++ b/solution.py
@@ -96,10 +96,6 @@
 
 def groups(planes, half):
     return [lambda k, block=block: pl.ds((k * half + block) * planes, planes) for block in range(half)]
-
-
-def edge_groups(planes, half):
-    return [lambda k, block=block: pl.ds((k * half + block) * planes, 1) for block in range(half)]
 
 
 def take(ref, rows, base=0):
@@ -190,14 +186,18 @@
 def edge_kernel(planes, half, step, block_ref, prefix_ref, pair_ref, seen_ref, raw_ref, here_ref, side_ref):
     flag = bit_of(step) == 1
     rows_of = 12 * half
-    for index, rows in enumerate(edge_groups(planes, half)):
-        poly, prefix = close(flag, take(block_ref, rows), take(prefix_ref, rows), take(seen_ref, rows))
-        partner = take(pair_ref, rows, rows_of * planes)
-        partner = pick(flag, times(take(seen_ref, rows), complete(partner)), partner)
-        row = lambda k: pl.ds(k * half + index, 1)
-        for ref, gauge in ((here_ref, prefix), (side_ref, partner)):
-            give(ref, row, poly)
-            give(ref, row, gauge, rows_of)
+
+    def plane(ref, base=0):
+        return matrix_at(lambda k: ref[pl.ds(base + k * half * planes, half, stride=planes), :], 2)
+
+    seen = plane(seen_ref)
+    poly, prefix = close(flag, plane(block_ref), plane(prefix_ref), seen)
+    partner = plane(pair_ref, rows_of * planes)
+    partner = pick(flag, times(seen, complete(partner)), partner)
+    rows = lambda k: pl.ds(k * half, half)
+    for ref, gauge in ((here_ref, prefix), (side_ref, partner)):
+        give(ref, rows, poly)
+        give(ref, rows, gauge, rows_of)
     here_ref[2 * rows_of:, :] = raw_ref[...]
 
 

time: 26.3 us -> 26.2 us (level)
  no operation moved by 1% of the time
where the time goes in v6:
time: 26.2 us; the launch traced here: 25.8 us
  starting transfers between devices  13 us (50%)
  Pallas kernels  6.2 us (24%)
  waiting for transfers between devices  5.95 us (23%)
  between operations  0.7 us (3%)
    ppermute x5, starting transfers between devices, across(): return lax.ppermute(x, 'ta', [(i, i ^ 1 << step) for i in range(times_ta)])  11.3 us
    ppermute x5, waiting for transfers between devices, across(): return lax.ppermute(x, 'ta', [(i, i ^ 1 << step) for i in range(times_ta)])  5.94 us
    pallas_call x2, Pallas kernels, product(): pl.pallas_call(functools.partial(block_kernel, half, which), out_shape=(s...  2.3 us
    pallas_call x1, Pallas kernels, on_device(): pl.pallas_call(functools.partial(last_kernel, half), out_shape=(shape(sli...  1.69 us
    ppermute x1, starting transfers between devices, on_device(): lax.ppermute(side, ('ta', 'gx'), [(i * parts_gx + j, (i ^ 1) * parts_gx +...  1.59 us
    pallas_call x1, Pallas kernels, on_device(): pl.pallas_call(functools.partial(late_kernel, planes, half, step), out_sh...  1.17 us
    pallas_call x1, Pallas kernels, on_device(): pl.pallas_call(functools.partial(early_kernel, planes, half, step), out_s...  0.78 us
  transfers between devices with their start and end apart: 7, of which 4 were waited for; matrix products, arithmetic and copies ran while one was open for 0% of the time, Pallas kernels for 12%

profile of v6, /device:TPU:0, one launch (start us, length us, event | category | flops | bytes accessed | tf_op | source)
XLA Modules:
  0.0 25.8 jit_solution(3809143340115232036)
XLA Ops:
  0.6 0.0 copy-start
  0.6 1.2 %block_product.3 = f32[192,128]{1,0:T(8,128)S(1)} custom-call(f32[2,4,18,8,512]{4,3,2,1,0:T(8,128)} %links_ref.5), custom_call_target="tpu_custom_call" | custom-call | flops 819200 | bytes 368640 | tf_op jit(solution)/shard_map/block_product/pallas_call | solution.py:383
  1.8 3.0 %collective-permute-start = (f32[192,128]{1,0:T(8,128)S(1)}, f32[192,128]{1,0:T(8,128)S(1)}, u32[]{:S(2)}, u32[]{:S(2)}) collective-permute-start(f32[192,128]{1,0:T(8,128)S(1)} %block_product.3), channel_id=1, source_target_pairs={{0,4},{4,0},{8,12},{12,8},{16,20},{20,16},{24,28},{28,24},{1,5},{5... | collective-permute-start | bytes 294920 | tf_op jit(solution)/shard_map/ppermute | solution.py:380
  4.9 1.1 %block_product.2 = (f32[192,128]{1,0:T(8,128)S(1)}, f32[48,128]{1,0:T(8,128)S(1)}) custom-call(f32[2,4,18,8,512]{4,3,2,1,0:T(8,128)} %links_ref.5), custom_call_target="tpu_custom_call" | custom-call | flops 819200 | bytes 368640 | tf_op jit(solution)/shard_map/block_product/pallas_call | solution.py:383
  6.0 1.7 %collective-permute-done.seen_ref = f32[192,128]{1,0:T(8,128)S(1)} collective-permute-done((f32[192,128]{1,0:T(8,128)S(1)}, f32[192,128]{1,0:T(8,128)S(1)}, u32[]{:S(2)}, u32[]{:S(2)}) %collective-permute-start) | collective-permute-done | bytes 98336 | tf_op jit(solution)/shard_map/ppermute | solution.py:380
  7.7 0.1 pair.1
  7.7 2.0 %collective-permute-start.1 = (f32[192,128]{1,0:T(8,128)S(1)}, f32[192,128]{1,0:T(8,128)S(1)}, u32[]{:S(2)}, u32[]{:S(2)}) collective-permute-start(f32[192,128]{1,0:T(8,128)S(1)} %get-tuple-element.18.refs_0_), channel_id=1, source_target_pairs={{0,8},{4,12},{8,0},{12,4},{16,24},{20,28},{24,16},{28,20},{1,9},{5... | collective-permute-start | bytes 294920 | tf_op jit(solution)/shard_map/ppermute | solution.py:380
  9.7 2.7 %collective-permute-done.1.refs_1_ = f32[192,128]{1,0:T(8,128)S(1)} collective-permute-done((f32[192,128]{1,0:T(8,128)S(1)}, f32[192,128]{1,0:T(8,128)S(1)}, u32[]{:S(2)}, u32[]{:S(2)}) %collective-permute-start.1) | collective-permute-done | bytes 98336 | tf_op jit(solution)/shard_map/ppermute | solution.py:380
  12.4 0.1 combine.1
  12.5 3.0 %collective-permute-start.2 = (f32[192,128]{1,0:T(8,128)S(1)}, f32[192,128]{1,0:T(8,128)S(1)}, u32[]{:S(2)}, u32[]{:S(2)}) collective-permute-start(f32[192,128]{1,0:T(8,128)S(1)} %get-tuple-element.20.block_ref), channel_id=1, source_target_pairs={{0,16},{4,20},{8,24},{12,28},{16,0},{20,4},{24,8},{28,12},{1,17},{... | collective-permute-start | bytes 294920 | tf_op jit(solution)/shard_map/ppermute | solution.py:380
  15.5 1.5 %collective-permute-start.5 = (f32[384,128]{1,0:T(8,128)S(1)}, f32[384,128]{1,0:T(8,128)S(1)}, u32[]{:S(2)}, u32[]{:S(2)}) collective-permute-start(f32[384,128]{1,0:T(8,128)S(1)} %get-tuple-element.22.pair_ref), channel_id=1, source_target_pairs={{0,4},{4,0},{8,12},{12,8},{16,20},{20,16},{24,28},{28,24},{1,5},{5... | collective-permute-start | bytes 589832 | tf_op jit(solution)/shard_map/ppermute | solution.py:380
  17.0 1.1 %collective-permute-done.2.seen_ref = f32[192,128]{1,0:T(8,128)S(1)} collective-permute-done((f32[192,128]{1,0:T(8,128)S(1)}, f32[192,128]{1,0:T(8,128)S(1)}, u32[]{:S(2)}, u32[]{:S(2)}) %collective-permute-start.2) | collective-permute-done | bytes 98336 | tf_op jit(solution)/shard_map/ppermute | solution.py:380
  18.1 1.8 %collective-permute-start.6 = (f32[192,128]{1,0:T(8,128)S(1)}, f32[192,128]{1,0:T(8,128)S(1)}, u32[]{:S(2)}, u32[]{:S(2)}) collective-permute-start(f32[192,128]{1,0:T(8,128)S(1)} %collective-permute-done.2.seen_ref), channel_id=1, source_target_pairs={{0,4},{4,0},{8,12},{12,8},{16,20},{20,16},{24,28},{28,24},{1,5},{5... | collective-permute-start | bytes 294920 | tf_op jit(solution)/shard_map/ppermute | solution.py:380
  19.9 0.1 edge.1
  20.0 0.1 collective-permute-start.3
  20.1 1.6 %collective-permute-start.4 = (f32[48,128]{1,0:T(8,128)S(1)}, f32[48,128]{1,0:T(8,128)S(1)}, u32[]{:S(2)}, u32[]{:S(2)}) collective-permute-start(f32[48,128]{1,0:T(8,128)S(1)} %get-tuple-element.25), channel_id=1, source_target_pairs={{0,7},{1,4},{2,5},{3,6},{4,3},{5,0},{6,1},{7,2},{8,15},{9,12},{10,... | collective-permute-start | bytes 73736 | tf_op jit(solution)/shard_map/ppermute | solution.py:439
  21.7 0.0 copy-done
  21.7 0.8 %early.1 = (f32[2,54,8,128]{3,2,1,0:T(8,128)S(1)}, f32[3,2,18,8,128]{4,3,2,1,0:T(8,128)S(1)}, f32[3,2,8,128]{3,2,1,0:T(8,128)S(1)}) custom-call(f32[2,4,18,8,512]{4,3,2,1,0:T(8,128)S(1)} %copy-done, f32[192,128]{1,0:T(8,128)S(1)} %get-tuple-element.20.block_ref, f32[192,128]{1,0:T(8,128)S(1)} %get-tuple-element.21.prefix_ref, ...), custom_call_target="tpu_custom_call" | custom-call | flops 4915200 | bytes 1638400 | tf_op jit(solution)/shard_map/early/pallas_call | solution.py:450
  22.5 0.5 %collective-permute-done.6.seen_ref = f32[192,128]{1,0:T(8,128)S(1)} collective-permute-done((f32[192,128]{1,0:T(8,128)S(1)}, f32[192,128]{1,0:T(8,128)S(1)}, u32[]{:S(2)}, u32[]{:S(2)}) %collective-permute-start.6) | collective-permute-done | bytes 98336 | tf_op jit(solution)/shard_map/ppermute | solution.py:380
  22.9 0.0 collective-permute-done.5.pair_ref
  22.9 1.2 %late.1 = (f32[2,54,8,128]{3,2,1,0:T(8,128)S(1)}, f32[5,2,18,8,128]{4,3,2,1,0:T(8,128)S(1)}, f32[5,2,8,128]{3,2,1,0:T(8,128)S(1)}) custom-call(f32[2,4,18,8,512]{4,3,2,1,0:T(8,128)S(1)} %copy-done, f32[384,128]{1,0:T(8,128)S(1)} %collective-permute-done.5.pair_ref, f32[192,128]{1,0:T(8,128)S(1)} %collective-permute-done.6.seen_ref, ...), custom_call_target="tpu_custom_call" | custom-call | flops 8192000 | bytes 2457600 | tf_op jit(solution)/shard_map/late/pallas_call | solution.py:459
  24.1 0.0 collective-permute-done.4.side_ref
  24.1 0.0 collective-permute-done.3.here_ref
  24.1 1.7 %last.1 = (f32[2,3,18,8,512]{4,3,2,1,0:T(8,128)}, f32[2,3,8,512]{3,2,1,0:T(8,128)}) custom-call(f32[2,4,18,8,512]{4,3,2,1,0:T(8,128)S(1)} %copy-done, f32[96,128]{1,0:T(8,128)S(1)} %collective-permute-done.3.here_ref, f32[48,128]{1,0:T(8,128)S(1)} %collective-permute-done.4.side_ref, f32[2,54,8,128]{3,2,1,0:T(8,128)S(1)} %get-tuple-element.26.field_own, ...), custom_call_target="tpu_custom_call" | custom-call | flops 6144000 | bytes 2457600 | tf_op jit(solution)/shard_map/last/pallas_call | solution.py:469
Async XLA Ops:
  0.6 21.1 %copy-start = (f32[2,4,18,8,512]{4,3,2,1,0:T(8,128)S(1)}, f32[2,4,18,8,512]{4,3,2,1,0:T(8,128)}, u32[]{:S(2)}) copy-start(f32[2,4,18,8,512]{4,3,2,1,0:T(8,128)} %links_ref.5) | copy-start | bytes 7077892
  1.8 5.8 %collective-permute-start = (f32[192,128]{1,0:T(8,128)S(1)}, f32[192,128]{1,0:T(8,128)S(1)}, u32[]{:S(2)}, u32[]{:S(2)}) collective-permute-start(f32[192,128]{1,0:T(8,128)S(1)} %block_product.3), channel_id=1, source_target_pairs={{0,4},{4,0},{8,12},{12,8},{16,20},{20,16},{24,28},{28,24},{1,5},{5... | collective-permute-start | bytes 294920 | tf_op jit(solution)/shard_map/ppermute | solution.py:380
  7.7 4.7 %collective-permute-start.1 = (f32[192,128]{1,0:T(8,128)S(1)}, f32[192,128]{1,0:T(8,128)S(1)}, u32[]{:S(2)}, u32[]{:S(2)}) collective-permute-start(f32[192,128]{1,0:T(8,128)S(1)} %get-tuple-element.18.refs_0_), channel_id=1, source_target_pairs={{0,8},{4,12},{8,0},{12,4},{16,24},{20,28},{24,16},{28,20},{1,9},{5... | collective-permute-start | bytes 294920 | tf_op jit(solution)/shard_map/ppermute | solution.py:380
  12.5 5.6 %collective-permute-start.2 = (f32[192,128]{1,0:T(8,128)S(1)}, f32[192,128]{1,0:T(8,128)S(1)}, u32[]{:S(2)}, u32[]{:S(2)}) collective-permute-start(f32[192,128]{1,0:T(8,128)S(1)} %get-tuple-element.20.block_ref), channel_id=1, source_target_pairs={{0,16},{4,20},{8,24},{12,28},{16,0},{20,4},{24,8},{28,12},{1,17},{... | collective-permute-start | bytes 294920 | tf_op jit(solution)/shard_map/ppermute | solution.py:380
  15.5 7.4 %collective-permute-start.5 = (f32[384,128]{1,0:T(8,128)S(1)}, f32[384,128]{1,0:T(8,128)S(1)}, u32[]{:S(2)}, u32[]{:S(2)}) collective-permute-start(f32[384,128]{1,0:T(8,128)S(1)} %get-tuple-element.22.pair_ref), channel_id=1, source_target_pairs={{0,4},{4,0},{8,12},{12,8},{16,20},{20,16},{24,28},{28,24},{1,5},{5... | collective-permute-start | bytes 589832 | tf_op jit(solution)/shard_map/ppermute | solution.py:380
  18.1 4.8 %collective-permute-start.6 = (f32[192,128]{1,0:T(8,128)S(1)}, f32[192,128]{1,0:T(8,128)S(1)}, u32[]{:S(2)}, u32[]{:S(2)}) collective-permute-start(f32[192,128]{1,0:T(8,128)S(1)} %collective-permute-done.2.seen_ref), channel_id=1, source_target_pairs={{0,4},{4,0},{8,12},{12,8},{16,20},{20,16},{24,28},{28,24},{1,5},{5... | collective-permute-start | bytes 294920 | tf_op jit(solution)/shard_map/ppermute | solution.py:380
  20.0 4.1 %collective-permute-start.3 = (f32[96,128]{1,0:T(8,128)S(1)}, f32[96,128]{1,0:T(8,128)S(1)}, u32[]{:S(2)}, u32[]{:S(2)}) collective-permute-start(f32[96,128]{1,0:T(8,128)S(1)} %get-tuple-element.24), channel_id=1, source_target_pairs={{0,3},{1,0},{2,1},{3,2},{4,7},{5,4},{6,5},{7,6},{8,11},{9,8},{10,9... | collective-permute-start | bytes 147464 | tf_op jit(solution)/shard_map/ppermute | solution.py:438
  20.1 4.0 %collective-permute-start.4 = (f32[48,128]{1,0:T(8,128)S(1)}, f32[48,128]{1,0:T(8,128)S(1)}, u32[]{:S(2)}, u32[]{:S(2)}) collective-permute-start(f32[48,128]{1,0:T(8,128)S(1)} %get-tuple-element.25), channel_id=1, source_target_pairs={{0,7},{1,4},{2,5},{3,6},{4,3},{5,0},{6,1},{7,2},{8,15},{9,12},{10,... | collective-permute-start | bytes 73736 | tf_op jit(solution)/shard_map/ppermute | solution.py:439
